TPU v7x, 16 devices: a whole 2x2x2 slice. The times are simulated.
16 devices in a mesh: model: 4 (over z, y), data: 4 (over x, core).
Axes of the slice: x: 2, y: 2, z: 2, core: 2. Of those that a mesh axis runs over, the one named last changes fastest.
Arguments:
- act_in: bfloat16 [32768, 1536], P('data')
- grad_out: bfloat16 [32768, 1536], P('data')
- w_up: bfloat16 [2, 1536, 6144], P(None, None, 'model')
- w_down: bfloat16 [2, 6144, 1536], P(None, 'model')
- master_up: float32 [2, 1536, 6144], P(None, 'data', 'model')
- master_down: float32 [2, 6144, 1536], P(None, ('model', 'data'))
- mom_up: float32 [2, 1536, 6144], P(None, 'data', 'model')
- mom_down: float32 [2, 6144, 1536], P(None, ('model', 'data'))
- var_up: float32 [2, 1536, 6144], P(None, 'data', 'model')
- var_down: float32 [2, 6144, 1536], P(None, ('model', 'data'))
- learn_rate: float32 [1], replicated
- clip_norm: float32 [1], replicated
Outputs:
- output 1: bfloat16 [2, 1536, 6144], P(None, None, 'model')
- output 2: bfloat16 [2, 6144, 1536], P(None, 'model')
- output 3: float32 [2, 1536, 6144], P(None, 'data', 'model')
- output 4: float32 [2, 6144, 1536], P(None, ('model', 'data'))
- output 5: float32 [2, 1536, 6144], P(None, 'data', 'model')
- output 6: float32 [2, 6144, 1536], P(None, ('model', 'data'))
- output 7: float32 [2, 1536, 6144], P(None, 'data', 'model')
- output 8: float32 [2, 6144, 1536], P(None, ('model', 'data'))
- output 9: float32 [1], replicated
All inputs are finite; a program needn't handle non-finite values.
Results may differ from a plain program's by a relative error of at most 0.00147203.
Values are sent between devices in bfloat16 or wider.
A program may use at most 1 GiB of HBM per device.

v0:
```python
import jax
import jax.numpy as jnp
from jax import lax
from jax.sharding import PartitionSpec as P

STEP = 10
BETA_ONE = 0.9
BETA_TWO = 0.95
ADAM_EPS = 1e-8
NORM_EPS = 1e-6


def gelu_fwd(z_low):
    return jax.nn.gelu(z_low.astype(jnp.float32)).astype(jnp.bfloat16)


def gelu_back(z_low, grad_low):
    _, back_fn = jax.vjp(jax.nn.gelu, z_low.astype(jnp.float32))
    return back_fn(grad_low.astype(jnp.float32))[0].astype(jnp.bfloat16)


def adam_update(master_arr, mom_arr, var_arr, grad_arr, clip_scale, lr_val):
    scaled = clip_scale * grad_arr
    new_mom = BETA_ONE * mom_arr + (1.0 - BETA_ONE) * scaled
    new_var = BETA_TWO * var_arr + (1.0 - BETA_TWO) * scaled * scaled
    mom_hat = new_mom / (1.0 - BETA_ONE ** STEP)
    var_hat = new_var / (1.0 - BETA_TWO ** STEP)
    new_master = master_arr - lr_val * mom_hat / (jnp.sqrt(var_hat) + ADAM_EPS)
    return new_master, new_mom, new_var


def local_grads(act_in, grad_out, w_up, w_down):
    z_one = jnp.dot(act_in, w_up[0], preferred_element_type=jnp.float32).astype(jnp.bfloat16)
    act_one = gelu_fwd(z_one)
    hid_part = jnp.dot(act_one, w_down[0], preferred_element_type=jnp.float32)
    hid_two = lax.psum(hid_part, "model").astype(jnp.bfloat16)
    z_two = jnp.dot(hid_two, w_up[1], preferred_element_type=jnp.float32).astype(jnp.bfloat16)
    act_two = gelu_fwd(z_two)
    grad_w4 = jnp.einsum("bf,bd->fd", act_two, grad_out, preferred_element_type=jnp.float32)
    dact_two = jnp.einsum("bd,fd->bf", grad_out, w_down[1], preferred_element_type=jnp.float32).astype(jnp.bfloat16)
    dz_two = gelu_back(z_two, dact_two)
    grad_w3 = jnp.einsum("bd,bf->df", hid_two, dz_two, preferred_element_type=jnp.float32)
    dhid_part = jnp.einsum("bf,df->bd", dz_two, w_up[1], preferred_element_type=jnp.float32)
    dhid_two = lax.psum(dhid_part, "model").astype(jnp.bfloat16)
    grad_w2 = jnp.einsum("bf,bd->fd", act_one, dhid_two, preferred_element_type=jnp.float32)
    dact_one = jnp.einsum("bd,fd->bf", dhid_two, w_down[0], preferred_element_type=jnp.float32).astype(jnp.bfloat16)
    dz_one = gelu_back(z_one, dact_one)
    grad_w1 = jnp.einsum("bd,bf->df", act_in, dz_one, preferred_element_type=jnp.float32)
    return grad_w1, grad_w3, grad_w2, grad_w4


def solution(mesh):
    data_size = mesh.shape["data"]
    spec_rows = P("data", None)
    spec_wup = P(None, None, "model")
    spec_wdown = P(None, "model", None)
    spec_sup = P(None, "data", "model")
    spec_sdown = P(None, ("model", "data"), None)
    spec_scalar = P(None)

    def local_step(act_in, grad_out, w_up, w_down, master_up, master_down, mom_up, mom_down, var_up, var_down, learn_rate, clip_norm):
        grad_w1, grad_w3, grad_w2, grad_w4 = local_grads(act_in, grad_out, w_up, w_down)
        shard_w4 = lax.psum_scatter(grad_w4, "data", scatter_dimension=0, tiled=True)
        shard_w3 = lax.psum_scatter(grad_w3, "data", scatter_dimension=0, tiled=True)
        shard_w2 = lax.psum_scatter(grad_w2, "data", scatter_dimension=0, tiled=True)
        shard_w1 = lax.psum_scatter(grad_w1, "data", scatter_dimension=0, tiled=True)
        grad_up = jnp.stack([shard_w1, shard_w3]) / data_size
        grad_down = jnp.stack([shard_w2, shard_w4]) / data_size
        sq_local = jnp.sum(grad_up * grad_up) + jnp.sum(grad_down * grad_down)
        norm_val = jnp.sqrt(lax.psum(sq_local, ("model", "data")))
        clip_scale = jnp.minimum(1.0, clip_norm[0] / (norm_val + NORM_EPS))
        lr_val = learn_rate[0]
        new_master_up, new_mom_up, new_var_up = adam_update(master_up, mom_up, var_up, grad_up, clip_scale, lr_val)
        new_master_down, new_mom_down, new_var_down = adam_update(master_down, mom_down, var_down, grad_down, clip_scale, lr_val)
        new_w_up = lax.all_gather(new_master_up.astype(jnp.bfloat16), "data", axis=1, tiled=True)
        new_w_down = lax.all_gather(new_master_down.astype(jnp.bfloat16), "data", axis=1, tiled=True)
        return (new_w_up, new_w_down, new_master_up, new_master_down, new_mom_up, new_mom_down, new_var_up, new_var_down, norm_val.reshape(1))

    return jax.shard_map(local_step, mesh=mesh, in_specs=(spec_rows, spec_rows, spec_wup, spec_wdown, spec_sup, spec_sdown, spec_sup, spec_sdown, spec_sup, spec_sdown, spec_scalar, spec_scalar), out_specs=(spec_wup, spec_wdown, spec_sup, spec_sdown, spec_sup, spec_sdown, spec_sup, spec_sdown, spec_scalar), check_vma=False)
```

profile of v0, /device:TPU:0, one launch (start us, length us, event | category | flops | bytes accessed | tf_op | source)
XLA Modules:
  0.0 4185.4 jit_solution(11873140095761726958)
XLA Ops:
  7.2 46.2 %convolution_convert_fusion.2 = bf16[8192,1536]{1,0:T(8,128)(2,1)} fusion(bf16[8192,1536]{1,0:T(8,128)(2,1)} %param.12, bf16[2,1536,1536]{2,1,0:T(8,128)(2,1)} %param.14), kind=kOutput, calls=%fused_computation.36 | convolution fusion | flops 38667288576 | bytes 55050240 | tf_op jit(solution)/shard_map/dot_general | solution.py:33
  53.4 51.8 %fusion.39 = f32[8192,1536]{1,0:T(8,128)} fusion(bf16[2,1536,1536]{2,1,0:T(8,128)(2,1)S(1)} %copy-done.1, bf16[8192,1536]{1,0:T(8,128)(2,1)} %convolution_convert_fusion.2), kind=kOutput, calls=%fused_computation.56 | convolution fusion | flops 38780534784 | bytes 80216064 | tf_op jit(solution)/shard_map/dot_general | solution.py:35
  105.2 1654.9 %all-reduce.2 = bf16[8192,1536]{1,0:T(8,128)(2,1)} all-reduce(f32[8192,1536]{1,0:T(8,128)} %fusion.39), channel_id=1, replica_groups=mesh['model'=4,'data'=4] {'model'}, use_global_device_ids=true, to_apply=%region_0.0 | all-reduce | flops 12582912 | bytes 75497472 | tf_op jit(solution)/shard_map/psum | solution.py:36
  1760.1 46.1 %convolution_convert_fusion.1 = bf16[8192,1536]{1,0:T(8,128)(2,1)} fusion(bf16[8192,1536]{1,0:T(8,128)(2,1)} %all-reduce.2, bf16[2,1536,1536]{2,1,0:T(8,128)(2,1)} %param.14), kind=kOutput, calls=%fused_computation.35 | convolution fusion | flops 38667288576 | bytes 55050240 | tf_op jit(solution)/shard_map/dot_general | solution.py:37
  1806.2 87.9 %fusion.4 = bf16[8192,1536]{1,0:T(8,128)(2,1)} fusion(bf16[8192,1536]{1,0:T(8,128)(2,1)} %convolution_convert_fusion.1, bf16[8192,1536]{1,0:T(8,128)(2,1)} %param.13, bf16[2,1536,1536]{2,1,0:T(8,128)(2,1)} %param.15), kind=kOutput, calls=%fused_computation.16 | convolution fusion | flops 38944112640 | bytes 80216064 | tf_op jit(solution)/shard_map/bd,fd->bf/dot_general | solution.py:40
  1894.1 48.4 %fusion.66 = f32[1536,1536]{0,1:T(8,128)} fusion(bf16[8192,1536]{1,0:T(8,128)(2,1)} %all-reduce.2, bf16[8192,1536]{1,0:T(8,128)(2,1)} %fusion.4), kind=kOutput, calls=%fused_computation.84 | convolution fusion | flops 38654705664 | bytes 59768832 | tf_op jit(solution)/shard_map/bd,bf->df/dot_general | solution.py:42
  1942.6 47.5 %fusion.34 = f32[8192,1536]{1,0:T(8,128)} fusion(bf16[8192,1536]{1,0:T(8,128)(2,1)} %fusion.4, bf16[2,1536,1536]{2,1,0:T(8,128)(2,1)} %param.14), kind=kOutput, calls=%fused_computation.52 | convolution fusion | flops 38654705664 | bytes 80216064 | tf_op jit(solution)/shard_map/bf,df->bd/dot_general | solution.py:43
  1990.1 1645.9 %all-reduce.3 = bf16[8192,1536]{1,0:T(8,128)(2,1)} all-reduce(f32[8192,1536]{1,0:T(8,128)} %fusion.34), channel_id=1, replica_groups=mesh['model'=4,'data'=4] {'model'}, use_global_device_ids=true, to_apply=%region_1.0 | all-reduce | flops 12582912 | bytes 75497472 | tf_op jit(solution)/shard_map/psum | solution.py:44
  3636.1 77.5 %fusion.7.clone.4 = bf16[8192,1536]{1,0:T(8,128)(2,1)} fusion(bf16[8192,1536]{1,0:T(8,128)(2,1)} %convolution_convert_fusion.2, bf16[8192,1536]{1,0:T(8,128)(2,1)} %all-reduce.3, bf16[2,1536,1536]{2,1,0:T(8,128)(2,1)} %param.15), kind=kOutput, calls=%fused_computation.19.clone.clone.clone.1 | convolution fusion | flops 38944112640 | bytes 80216064 | tf_op jit(solution)/shard_map/bd,fd->bf/dot_general | solution.py:46
  3713.6 48.5 %convolution_bitcast_fusion = f32[1536,1536]{0,1:T(8,128)} fusion(bf16[8192,1536]{1,0:T(8,128)(2,1)} %param.12, bf16[8192,1536]{1,0:T(8,128)(2,1)} %fusion.7.clone.4), kind=kOutput, calls=%fused_computation.45 | convolution fusion | flops 38654705664 | bytes 59768832 | tf_op jit(solution)/shard_map/bd,bf->df/dot_general | solution.py:48
  3762.1 49.9 %fusion.22 = f32[1536,1536]{0,1:T(8,128)} fusion(bf16[8192,1536]{1,0:T(8,128)(2,1)} %param.13, bf16[8192,1536]{1,0:T(8,128)(2,1)} %convolution_convert_fusion.1), kind=kOutput, calls=%fused_computation.38 | convolution fusion | flops 38780534784 | bytes 59768832 | tf_op jit(solution)/shard_map/bf,bd->fd/dot_general | solution.py:39
  3812.1 49.8 %fusion.24 = f32[1536,1536]{0,1:T(8,128)} fusion(bf16[8192,1536]{1,0:T(8,128)(2,1)} %all-reduce.3, bf16[8192,1536]{1,0:T(8,128)(2,1)} %convolution_convert_fusion.2), kind=kOutput, calls=%fused_computation.39 | convolution fusion | flops 38780534784 | bytes 59768832 | tf_op jit(solution)/shard_map/bf,bd->fd/dot_general | solution.py:45
  3862.0 6.3 copy.26
  3869.6 6.0 copy.21
  3875.6 6.0 copy.25
  3885.9 25.6 reduce-scatter.11.cloned.1.call-done
  3911.5 75.8 %reduce-scatter.9.cloned.1.call-done = f32[384,1536]{0,1:T(8,128)} async-done(((f32[1536,1536]{0,1:T(8,128)}), f32[384,1536]{0,1:T(8,128)}) %reduce-scatter.9.cloned.1.call-update) | async-done | bytes 2359312 | tf_op jit(solution)/shard_map/reduce_scatter | solution.py:65
  3992.8 31.8 psum.23
  4025.3 11.5 fusion.64
  4036.9 6.0 copy.29
  4043.0 6.0 copy.27
  4049.0 6.0 copy.28
  4055.0 10.9 fusion.62
  4066.0 6.0 copy.32
  4072.0 6.0 copy.33
  4078.1 6.0 copy.34
  4084.1 6.0 copy.35
  4090.1 6.0 copy.36
  4096.2 6.1 copy.37
  4102.2 12.6 copy.30
  4114.8 49.5 %all-gather.5.cloned.1.call-done = bf16[2,1536,1536]{1,2,0:T(8,128)(2,1)} async-done(((bf16[2,384,1536]{1,2,0:T(8,128)(2,1)}), bf16[2,1536,1536]{1,2,0:T(8,128)(2,1)}) %all-gather.5.cloned.1.call-update) | async-done | bytes 9437200 | tf_op jit(solution)/shard_map/all_gather | solution.py:76
  4164.4 12.6 copy.31
  (21 shorter events, 8.7 us)
Async XLA Ops:
  7.2 3874.5 %reduce-scatter.7.cloned.1.call-start = ((), (), s32[]{:S(2)}) async-start(), calls=%async_computation.5 | async-start | bytes 11796480 | tf_op jit(solution)/shard_map/reduce_scatter | solution.py:64
  7.2 46.2 %copy-start.1 = (bf16[2,1536,1536]{2,1,0:T(8,128)(2,1)S(1)}, bf16[2,1536,1536]{2,1,0:T(8,128)(2,1)}, u32[]{:S(2)}) copy-start(bf16[2,1536,1536]{2,1,0:T(8,128)(2,1)} %param.15) | copy-start | bytes 28311556
  1942.6 1939.1 %reduce-scatter.5.cloned.1.call-start = ((), (), s32[]{:S(2)}) async-start(), calls=%async_computation.4 | async-start | bytes 11796480 | tf_op jit(solution)/shard_map/reduce_scatter | solution.py:66
  3762.1 149.4 %reduce-scatter.11.cloned.1.call-start = ((), (), s32[]{:S(2)}) async-start(), calls=%async_computation.7 | async-start | bytes 11796480 | tf_op jit(solution)/shard_map/reduce_scatter | solution.py:63
  3812.1 175.2 %reduce-scatter.9.cloned.1.call-start = ((), (), s32[]{:S(2)}) async-start(), calls=%async_computation.6 | async-start | bytes 11796480 | tf_op jit(solution)/shard_map/reduce_scatter | solution.py:65
  3861.9 240.3 %all-gather.3.cloned.1.call-start = ((), (), s32[]{:S(2)}) async-start(), calls=%async_computation.8 | async-start | bytes 11796480 | tf_op jit(solution)/shard_map/all_gather | solution.py:75
  4025.3 29.7 copy-start
  4036.9 127.5 %all-gather.5.cloned.1.call-start = ((), (), s32[]{:S(2)}) async-start(), calls=%async_computation.9 | async-start | bytes 11796480 | tf_op jit(solution)/shard_map/all_gather | solution.py:76
Sparse Core Ops, SparseCore 0:
  1942.7 73.8 reduce-scatter.6
  3762.2 73.2 reduce-scatter.4
  3838.1 73.3 reduce-scatter.10
  3913.9 73.3 reduce-scatter.8
  4037.0 63.3 all-gather.2
  4101.8 62.5 all-gather.4
where the time goes:
time: 4190 us
  blocking collectives  3330 us (79%)
  matrix products  554 us (13%)
  waiting for transfers between devices  151 us (4%)
  local copies, waits for them, and re-layouts  98 us (2%)
    psum x1, blocking collectives, local_grads(): hid_two = lax.psum(hid_part, 'model').astype(jnp.bfloat16)  1650 us
    psum x1, blocking collectives, local_grads(): dhid_two = lax.psum(dhid_part, 'model').astype(jnp.bfloat16)  1650 us
    unnamed x18, local copies, waits for them, and re-layouts  98 us
    dot_general x1, matrix products, local_grads(): jnp.einsum('bd,fd->bf', grad_out, w_down[1], preferred_element_type=jnp.f...  87.9 us
  transfers between devices with their start and end apart: 6, of which 3 were waited for; matrix products, arithmetic and copies ran while one was open for 9% of the time, Pallas kernels for 0%

commit v1 on v0

v1 whole, which is shorter than its diff:
```python
import jax
import jax.numpy as jnp
from jax import lax
from jax.experimental import pallas as pl
from jax.experimental.pallas import tpu as pltpu
from jax.sharding import Mesh, PartitionSpec as P


STEP = 10
BETA_ONE = 0.9
BETA_TWO = 0.95
ADAM_EPS = 1e-8
NORM_EPS = 1e-6
DATA = 4


def gelu_fwd(z_low):
    return jax.nn.gelu(z_low.astype(jnp.float32)).astype(jnp.bfloat16)


def gelu_back(z_low, grad_low):
    _, back_fn = jax.vjp(jax.nn.gelu, z_low.astype(jnp.float32))
    return back_fn(grad_low.astype(jnp.float32))[0].astype(jnp.bfloat16)


def adam_kernel(scale_ref, lr_ref, master_ref, mom_ref, var_ref, grad_ref, *refs):
    out_master, out_mom, out_var, out_low = refs[-4:]
    scaled = scale_ref[0] * (grad_ref[...] / DATA)
    new_mom = BETA_ONE * mom_ref[0] + (1.0 - BETA_ONE) * scaled
    new_var = BETA_TWO * var_ref[0] + (1.0 - BETA_TWO) * scaled * scaled
    mom_hat = new_mom / (1.0 - BETA_ONE ** STEP)
    var_hat = new_var / (1.0 - BETA_TWO ** STEP)
    new_master = master_ref[0] - lr_ref[0] * mom_hat / (jnp.sqrt(var_hat) + ADAM_EPS)
    out_master[0], out_mom[0], out_var[0] = new_master, new_mom, new_var
    out_low[...] = new_master.astype(jnp.bfloat16)


def adam_update(layer, scale, lr_val, master, mom, var, grad, earlier):
    rows, cols = grad.shape
    tile = rows // 6
    smem = pl.BlockSpec(memory_space=pltpu.SMEM)
    slab = pl.BlockSpec((1, tile, cols), lambda i: (layer, i, 0))
    flat = pl.BlockSpec((tile, cols), lambda i: (i, 0))
    held = [pl.BlockSpec(memory_space=pl.ANY)] * len(earlier)
    count = master[0].size
    return pl.pallas_call(
        adam_kernel,
        grid=(6,),
        out_shape=[jax.ShapeDtypeStruct(master.shape, jnp.float32)] * 3 + [jax.ShapeDtypeStruct(grad.shape, jnp.bfloat16)],
        in_specs=[smem, smem, slab, slab, slab, flat] + held,
        out_specs=[slab, slab, slab, flat],
        input_output_aliases={6 + i: i for i in range(len(earlier))},
        cost_estimate=pl.CostEstimate(flops=20 * count, bytes_accessed=30 * count, transcendentals=count),
        name="adam",
    )(scale, lr_val, master, mom, var, grad, *earlier)


def swap(arr, axis):
    return lax.ppermute(arr, axis, [(0, 1), (1, 0)])


def gather_model(block):
    z_pos, y_pos, block = lax.optimization_barrier((lax.axis_index("z"), lax.axis_index("y"), block))
    half = block.shape[0] // 2
    top, bot = block[:half], block[half:]
    top_z, bot_y = swap(top, "z"), swap(bot, "y")
    top_y, bot_z = swap(top, "y"), swap(bot, "z")
    top_zy, bot_zy = swap(top_z, "y"), swap(bot_y, "z")
    rows, _ = block.shape
    full = jnp.concatenate([block] * 4, 0)
    for dz, dy, upper, lower in ((1, 0, top_z, bot_z), (0, 1, top_y, bot_y), (1, 1, top_zy, bot_zy)):
        place = 2 * (z_pos ^ dz) + (y_pos ^ dy)
        full = lax.dynamic_update_slice(full, upper, (place * rows, 0))
        full = lax.dynamic_update_slice(full, lower, (place * rows + half, 0))
    return full


def dot(left, right, dims):
    return lax.dot_general(left, right, (dims, ((), ())), preferred_element_type=jnp.float32)


def core_sum(part_own, part_oth):
    from_oth = swap(part_oth, "c")
    own = (lax.optimization_barrier(part_own) + from_oth).astype(jnp.bfloat16)
    return own, swap(own, "c")


def solution(mesh):
    mesh = Mesh(mesh.devices.reshape(2, 2, 2, 2), ("z", "y", "x", "c"))
    model, data = ("z", "y"), ("x", "c")
    spec_rows = P(data, None)
    spec_wup = P(None, None, model)
    spec_wdown = P(None, model, None)
    spec_sup = P(None, data, model)
    spec_sdown = P(None, model + data, None)
    spec_scalar = P(None)

    def whole_step(act_in, grad_out, w_up, w_down, master_up, master_down, mom_up, mom_down, var_up, var_down, learn_rate, clip_norm):
        core, x_pos = lax.axis_index("c"), lax.axis_index("x")
        quarter = 2 * lax.axis_index("z") + lax.axis_index("y")
        rows = act_in.shape[0] // 4
        dim = act_in.shape[1]
        piece = dim // 4

        def up_block(layer):
            parts = [lax.dynamic_slice(w_up, (layer, 0, (2 * i + core) * piece), (1, dim, piece))[0].T for i in range(2)]
            return jnp.concatenate(parts, 0)

        def down_block(layer):
            parts = [lax.dynamic_slice(w_down, (layer, (2 * i + core) * piece, 0), (1, piece, dim))[0] for i in range(2)]
            return jnp.concatenate(parts, 0)

        w_one = gather_model(up_block(0))
        x_own = lax.dynamic_slice_in_dim(act_in, quarter * rows, rows, 0)
        dy_own = lax.dynamic_slice_in_dim(grad_out, quarter * rows, rows, 0)
        x_oth, dy_oth = swap(x_own, "c"), swap(dy_own, "c")
        x_all = jnp.concatenate([x_own, x_oth], 0)
        dy_all = jnp.concatenate([dy_own, dy_oth], 0)
        w_two = gather_model(down_block(0))
        w_three = gather_model(up_block(1))
        w_four = gather_model(down_block(1))

        z_one_oth = dot(x_oth, w_one, ((1,), (1,))).astype(jnp.bfloat16)
        act_one_oth = gelu_fwd(z_one_oth)
        z_one_own = dot(x_own, w_one, ((1,), (1,))).astype(jnp.bfloat16)
        act_one_own = gelu_fwd(z_one_own)
        hid_oth = dot(act_one_oth, w_two, ((1,), (0,)))
        hid_own = dot(act_one_own, w_two, ((1,), (0,)))
        z_one = jnp.concatenate([z_one_own, z_one_oth], 0)
        act_one = jnp.concatenate([act_one_own, act_one_oth], 0)
        hid_own, hid_oth = core_sum(hid_own, hid_oth)
        hid_two = jnp.concatenate([hid_own, hid_oth], 0)
        z_two = dot(hid_two, w_three, ((1,), (1,))).astype(jnp.bfloat16)
        act_two = gelu_fwd(z_two)

        def scatter(grad):
            return lax.psum_scatter(grad, ("z", "y", "x"), scatter_dimension=0, tiled=True)

        def model_major(grad):
            return grad.reshape(dim, 4, 2 * piece).transpose(1, 0, 2).reshape(4 * dim, 2 * piece)

        def core_exchange(mine):
            mine = mine.reshape(2, piece, 2, piece)
            keep = lax.dynamic_index_in_dim(mine, core, 0, keepdims=False)
            give = lax.dynamic_index_in_dim(mine, 1 - core, 0, keepdims=False)
            got = swap(give, "c")
            pair = jnp.where(core == 0, jnp.stack([keep, got], 2), jnp.stack([got, keep], 2))
            return pair.reshape(piece, dim)

        grad_w4 = dot(act_two, dy_all, ((0,), (0,)))
        sum_w4 = scatter(grad_w4)
        dact_two = dot(dy_all, w_four, ((1,), (1,))).astype(jnp.bfloat16)
        dz_two = gelu_back(z_two, dact_two)
        grad_w3 = dot(hid_two, dz_two, ((0,), (0,)))
        sum_w3 = scatter(model_major(grad_w3))
        dhid_oth = dot(dz_two[rows:], w_three, ((1,), (0,)))
        dhid_own = dot(dz_two[:rows], w_three, ((1,), (0,)))
        dhid_own, dhid_oth = core_sum(dhid_own, dhid_oth)
        dhid_two = jnp.concatenate([dhid_own, dhid_oth], 0)
        grad_w2 = dot(act_one, dhid_two, ((0,), (0,)))
        sum_w2 = scatter(grad_w2)
        dact_one = dot(dhid_two, w_two, ((1,), (1,))).astype(jnp.bfloat16)
        dz_one = gelu_back(z_one, dact_one)
        grad_w1 = dot(x_all, dz_one, ((0,), (0,)))
        sum_w1 = scatter(model_major(grad_w1))

        total = jnp.zeros((1,), jnp.float32)
        for part in (sum_w4, sum_w3, sum_w2, sum_w1):
            total = total + jnp.sum((part / DATA) * (part / DATA))
        for axis in ("c", "x", "y", "z"):
            total = total + swap(total, axis)
        norm_val = jnp.sqrt(total)
        clip_scale = jnp.minimum(1.0, clip_norm[0] / (norm_val[0] + NORM_EPS))
        sum_w1, sum_w3 = core_exchange(sum_w1), core_exchange(sum_w3)

        new_w_up = jnp.zeros((2, dim, dim), jnp.bfloat16)
        new_w_down = jnp.zeros((2, dim, dim), jnp.bfloat16)
        scale = clip_scale.reshape(1)
        up, down = (), ()
        for name, layer, grad in (("down", 1, sum_w4), ("up", 1, sum_w3), ("down", 0, sum_w2), ("up", 0, sum_w1)):
            if name == "up":
                *up, low = adam_update(layer, scale, learn_rate, master_up, mom_up, var_up, grad, up)
            else:
                *down, low = adam_update(layer, scale, learn_rate, master_down, mom_down, var_down, grad, down)
            far = swap(low, "x")
            near, far_near = swap(low, "c"), swap(far, "c")
            for dx, dc, part in ((0, 0, low), (0, 1, near), (1, 0, far), (1, 1, far_near)):
                place = (layer, (2 * (x_pos ^ dx) + (core ^ dc)) * piece, 0)
                if name == "up":
                    new_w_up = lax.dynamic_update_slice(new_w_up, part[None], place)
                else:
                    new_w_down = lax.dynamic_update_slice(new_w_down, part[None], place)
        (new_master_up, new_mom_up, new_var_up), (new_master_down, new_mom_down, new_var_down) = up, down
        return (new_w_up, new_w_down, new_master_up, new_master_down, new_mom_up, new_mom_down, new_var_up, new_var_down, norm_val)

    return jax.shard_map(whole_step, mesh=mesh, in_specs=(spec_rows, spec_rows, spec_wup, spec_wdown, spec_sup, spec_sdown, spec_sup, spec_sdown, spec_sup, spec_sdown, spec_scalar, spec_scalar), out_specs=(spec_wup, spec_wdown, spec_sup, spec_sdown, spec_sup, spec_sdown, spec_sup, spec_sdown, spec_scalar), check_vma=False)
```

time: 4190 us -> 1350 us (0.32)
  blocking collectives: 3330 us -> 0 us
  waiting for transfers between devices: 151 us -> 492 us
  local copies, waits for them, and re-layouts: 98 us -> 142 us
  starting transfers between devices: 0.25 us -> 44.2 us
    psum x3 -> x0, blocking collectives: 3330 us -> none  [the longest x1 1650 us: local_grads(): hid_two = lax.psum(hid_part, 'model').astype(jnp.bfloat16)]
    ppermute x0 -> x48, waiting for transfers between devices: none -> 244 us  [swap(): return lax.ppermute(arr, axis, [(0, 1), (1, 0)])]
    reduce_scatter x4, waiting for transfers between devices: 101 us -> 248 us  [scatter(): lax.psum_scatter(grad, ('z', 'y', 'x'), scatter_dimension=0, tiled=True)]
    unnamed x18 -> x24, local copies, waits for them, and re-layouts: 98 us -> 1.45 us
    dynamic_update_slice x0 -> x40, local copies, waits for them, and re-layouts: none -> 57.1 us  [the longest x12 17.3 us: gather_model(): full = lax.dynamic_update_slice(full, lower, (place * rows + half, 0))]
    all_gather x2 -> x0, waiting for transfers between devices: 49.5 us -> none  [the longest x1 49.5 us: local_step(): lax.all_gather(new_master_down.astype(jnp.bfloat16), 'data', axis=1, tile...]
    ppermute x0 -> x48, starting transfers between devices: none -> 44.1 us  [swap(): return lax.ppermute(arr, axis, [(0, 1), (1, 0)])]
    dot_general x10 -> x13, matrix products: 554 us -> 549 us  [dot(): lax.dot_general(left, right, (dims, ((), ())), preferred_element_type=jnp...]
  transfers between devices with their start and end apart: 6 -> 52, of which waited for: 3 -> 20; matrix products, arithmetic and copies ran while one was open for 9% -> 41% of each run, Pallas kernels for 0% -> 2%
where the time goes in v1:
time: 1350 us
  matrix products  549 us (41%)
  waiting for transfers between devices  492 us (36%)
  local copies, waits for them, and re-layouts  142 us (11%)
  other arithmetic  65.1 us (5%)
  starting transfers between devices  44.2 us (3%)
  Pallas kernels  32.4 us (2%)
  between operations  22 us (2%)
    dot_general x13, matrix products, dot(): lax.dot_general(left, right, (dims, ((), ())), preferred_element_type=jnp...  549 us
    reduce_scatter x4, waiting for transfers between devices, scatter(): lax.psum_scatter(grad, ('z', 'y', 'x'), scatter_dimension=0, tiled=True)  248 us
    ppermute x48, waiting for transfers between devices, swap(): return lax.ppermute(arr, axis, [(0, 1), (1, 0)])  244 us
    ppermute x48, starting transfers between devices, swap(): return lax.ppermute(arr, axis, [(0, 1), (1, 0)])  44.1 us
    pallas_call x4, Pallas kernels, adam_update(): pl.pallas_call(adam_kernel, grid=(6,), out_shape=[jax.ShapeDtypeStruct(ma...  32.4 us
    reshape x2, local copies, waits for them, and re-layouts, model_major(): grad.reshape(dim, 4, 2 * piece).transpose(1, 0, 2)  29.8 us
  transfers between devices with their start and end apart: 52, of which 20 were waited for; matrix products, arithmetic and copies ran while one was open for 41% of the time, Pallas kernels for 2%

profile of v1, /device:TPU:0, one launch (start us, length us, event | category | flops | bytes accessed | tf_op | source)
XLA Modules:
  0.0 1347.3 jit_solution(7141912511828192271)
XLA Ops:
  35.8 8.1 collective-permute-done
  45.9 23.4 %collective-permute-done.1 = bf16[384,1536]{0,1:T(8,128)(2,1)} collective-permute-done((bf16[384,1536]{0,1:T(8,128)(2,1)}, bf16[384,1536]{0,1:T(8,128)(2,1)}, u32[]{:S(2)}, u32[]{:S(2)}) %collective-permute-start.1) | collective-permute-done | bytes 1179680 | tf_op jit(solution)/shard_map/ppermute | solution.py:59
  83.3 11.2 collective-permute-done.6
  98.9 20.1 %collective-permute-done.7 = bf16[384,1536]{1,0:T(8,128)(2,1)} collective-permute-done((bf16[384,1536]{1,0:T(8,128)(2,1)}, bf16[384,1536]{1,0:T(8,128)(2,1)}, u32[]{:S(2)}, u32[]{:S(2)}) %collective-permute-start.7) | collective-permute-done | bytes 1179680 | tf_op jit(solution)/shard_map/ppermute | solution.py:59
  129.9 25.0 %collective-permute-done.4 = bf16[384,1536]{0,1:T(8,128)(2,1)S(1)} collective-permute-done((bf16[384,1536]{0,1:T(8,128)(2,1)S(1)}, bf16[384,1536]{0,1:T(8,128)(2,1)S(1)}, u32[]{:S(2)}, u32[]{:S(2)}) %collective-permute-start.4) | collective-permute-done | bytes 1179680 | tf_op jit(solution)/shard_map/ppermute | solution.py:59
  157.2 19.6 %collective-permute-done.10 = bf16[384,1536]{1,0:T(8,128)(2,1)S(1)} collective-permute-done((bf16[384,1536]{1,0:T(8,128)(2,1)}, bf16[384,1536]{1,0:T(8,128)(2,1)S(1)}, u32[]{:S(2)}, u32[]{:S(2)}) %collective-permute-start.10) | collective-permute-done | bytes 1179680 | tf_op jit(solution)/shard_map/ppermute | solution.py:59
  177.1 36.5 %fusion.32 = (bf16[2048,3072]{1,0:T(8,128)(2,1)}, bf16[2048,3072]{1,0:T(8,128)(2,1)}) fusion(bf16[2048,1536]{1,0:T(8,128)(2,1)} %collective-permute-done.12, bf16[3072,1536]{0,1:T(8,128)(2,1)} %constant_dynamic-update-slice_fusion.18), kind=kOutput, calls=%fused_computation.51 | convolution fusion | flops 19396558848 | bytes 40894464 | tf_op jit(solution)/shard_map/dot_general | solution.py:79
  213.6 24.0 %fusion.72 = f32[2048,1536]{1,0:T(8,128)} fusion(bf16[2048,3072]{1,0:T(8,128)(2,1)} %get-tuple-element.87, bf16[3072,1536]{1,0:T(8,128)(2,1)S(1)} %constant_dynamic-update-slice_fusion.12), kind=kOutput, calls=%fused_computation.167 | convolution fusion | flops 19327352832 | bytes 34603008 | tf_op jit(solution)/shard_map/dot_general | solution.py:79
  243.4 33.2 %fusion.26 = (bf16[2048,3072]{1,0:T(8,128)(2,1)}, bf16[2048,3072]{1,0:T(8,128)(2,1)}) fusion(bf16[2048,1536]{1,0:T(8,128)(2,1)} %constant_dynamic-slice_fusion.3, bf16[3072,1536]{0,1:T(8,128)(2,1)} %constant_dynamic-update-slice_fusion.18), kind=kOutput, calls=%fused_computation.45 | convolution fusion | flops 19396558848 | bytes 40894464 | tf_op jit(solution)/shard_map/dot_general | solution.py:79
  276.6 24.3 %fusion.71 = f32[2048,1536]{1,0:T(8,128)S(1)} fusion(bf16[2048,3072]{1,0:T(8,128)(2,1)} %get-tuple-element.85, bf16[3072,1536]{1,0:T(8,128)(2,1)} %copy-done.4), kind=kOutput, calls=%fused_computation.166 | convolution fusion | flops 19327352832 | bytes 34603008 | tf_op jit(solution)/shard_map/dot_general | solution.py:79
  332.7 13.3 collective-permute-done.22
  349.9 20.9 %collective-permute-done.23 = bf16[384,1536]{1,0:T(8,128)(2,1)} collective-permute-done((bf16[384,1536]{1,0:T(8,128)(2,1)}, bf16[384,1536]{1,0:T(8,128)(2,1)}, u32[]{:S(2)}, u32[]{:S(2)}) %collective-permute-start.23) | collective-permute-done | bytes 1179680 | tf_op jit(solution)/shard_map/ppermute | solution.py:59
  381.9 22.5 %collective-permute-done.19 = bf16[384,1536]{0,1:T(8,128)(2,1)S(1)} collective-permute-done((bf16[384,1536]{0,1:T(8,128)(2,1)S(1)}, bf16[384,1536]{0,1:T(8,128)(2,1)S(1)}, u32[]{:S(2)}, u32[]{:S(2)}) %collective-permute-start.19) | collective-permute-done | bytes 1179680 | tf_op jit(solution)/shard_map/ppermute | solution.py:59
  405.1 23.5 %collective-permute-done.26 = bf16[384,1536]{1,0:T(8,128)(2,1)S(1)} collective-permute-done((bf16[384,1536]{1,0:T(8,128)(2,1)}, bf16[384,1536]{1,0:T(8,128)(2,1)S(1)}, u32[]{:S(2)}, u32[]{:S(2)}) %collective-permute-start.26) | collective-permute-done | bytes 1179680 | tf_op jit(solution)/shard_map/ppermute | solution.py:59
  430.9 44.7 %convolution_convert_fusion = bf16[4096,3072]{1,0:T(8,128)(2,1)} fusion(bf16[3072,1536]{0,1:T(8,128)(2,1)S(1)} %constant_dynamic-update-slice_fusion.6, bf16[2048,1536]{1,0:T(8,128)(2,1)} %collective-permute-done.14, bf16[2048,1536]{1,0:T(8,128)(2,1)} %add_convert_fusion.1), kind=kOutput, calls=%fused_computation.58 | convolution fusion | flops 38692454400 | bytes 47185920 | tf_op jit(solution)/shard_map/dot_general | solution.py:79
  475.6 73.1 %fusion.4 = bf16[4096,3072]{1,0:T(8,128)(2,1)} fusion(bf16[4096,3072]{1,0:T(8,128)(2,1)} %convolution_convert_fusion, bf16[3072,1536]{1,0:T(8,128)(2,1)} %constant_dynamic-update-slice_fusion, bf16[2048,1536]{1,0:T(8,128)(2,1)} %collective-permute-done.21, bf16[2048,1536]{1,0:T(8,128)(2,1)} %constant_dynamic-slice_fusion.2), kind=kOutput, calls=%fused_computation.15 | convolution fusion | flops 38969278464 | bytes 72351744 | tf_op jit(solution)/shard_map/dot_general | solution.py:79
  548.7 48.9 %fusion.49 = f32[1536,3072]{1,0:T(8,128)} fusion(bf16[4096,3072]{1,0:T(8,128)(2,1)} %fusion.4, bf16[2048,1536]{1,0:T(8,128)(2,1)} %collective-permute-done.14, bf16[2048,1536]{1,0:T(8,128)(2,1)} %add_convert_fusion.1), kind=kOutput, calls=%fused_computation.80 | convolution fusion | flops 38679871488 | bytes 56623104 | tf_op jit(solution)/shard_map/dot_general | solution.py:79
  597.6 14.5 %copy.34 = f32[192,4,8,768]{3,2,0,1:T(8,128)} copy(f32[192,4,8,768]{3,2,1,0:T(8,128)} %bitcast.94) | data formatting | bytes 37748736 | tf_op jit(solution)/shard_map/reshape | solution.py:140
  612.2 26.6 %fusion.41 = f32[2048,1536]{1,0:T(8,128)} fusion(bf16[3072,1536]{0,1:T(8,128)(2,1)} %copy-done.6, bf16[4096,3072]{1,0:T(8,128)(2,1)} %fusion.4), kind=kOutput, calls=%fused_computation.61 | convolution fusion | flops 19327352832 | bytes 34603008 | tf_op jit(solution)/shard_map/dot_general | solution.py:79
  638.8 56.8 %fusion.37 = f32[3072,1536]{1,0:T(8,128)} fusion(bf16[4096,3072]{1,0:T(8,128)(2,1)} %convolution_convert_fusion, bf16[2048,1536]{1,0:T(8,128)(2,1)} %collective-permute-done.21, bf16[2048,1536]{1,0:T(8,128)(2,1)} %constant_dynamic-slice_fusion.2), kind=kOutput, calls=%fused_computation.56 | convolution fusion | flops 38805700608 | bytes 56623104 | tf_op jit(solution)/shard_map/dot_general | solution.py:79
  695.7 25.0 %fusion.43 = f32[2048,1536]{1,0:T(8,128)S(1)} fusion(bf16[3072,1536]{0,1:T(8,128)(2,1)} %copy-done.6, bf16[4096,3072]{1,0:T(8,128)(2,1)} %fusion.4), kind=kOutput, calls=%fused_computation.63 | convolution fusion | flops 19327352832 | bytes 34603008 | tf_op jit(solution)/shard_map/dot_general | solution.py:79
  727.6 12.4 fusion.100
  740.1 47.5 %fusion.48 = bf16[4096,3072]{1,0:T(8,128)(2,1)} fusion(bf16[3072,1536]{1,0:T(8,128)(2,1)} %copy-done.4, bf16[2048,1536]{1,0:T(8,128)(2,1)} %collective-permute-done.29, bf16[2048,1536]{1,0:T(8,128)(2,1)} %copy-done.8), kind=kOutput, calls=%fused_computation.79 | convolution fusion | flops 38679871488 | bytes 47185920 | tf_op jit(solution)/shard_map/dot_general | solution.py:79
  787.6 57.3 %fusion.39 = f32[1536,3072]{1,0:T(8,128)} fusion(bf16[2048,3072]{1,0:T(8,128)(2,1)} %get-tuple-element.88, bf16[2048,3072]{1,0:T(8,128)(2,1)} %get-tuple-element.86, bf16[4096,3072]{1,0:T(8,128)(2,1)} %fusion.48, bf16[4096,1536]{1,0:T(8,128)(2,1)} %fusion.100), kind=kOutput, calls=%fused_computation.57 | convolution fusion | flops 38969278464 | bytes 81788928 | tf_op jit(solution)/shard_map/dot_general | solution.py:79
  844.9 15.3 %copy.33 = f32[192,4,8,768]{3,2,0,1:T(8,128)} copy(f32[192,4,8,768]{3,2,1,0:T(8,128)} %bitcast.93) | data formatting | bytes 37748736 | tf_op jit(solution)/shard_map/reshape | solution.py:140
  860.3 51.2 %fusion.33 = f32[3072,1536]{1,0:T(8,128)} fusion(bf16[2048,3072]{1,0:T(8,128)(2,1)} %get-tuple-element.87, bf16[2048,3072]{1,0:T(8,128)(2,1)} %get-tuple-element.85, bf16[2048,1536]{1,0:T(8,128)(2,1)} %collective-permute-done.29, bf16[2048,1536]{1,0:T(8,128)(2,1)} %copy-done.8), kind=kOutput, calls=%fused_computation.52 | convolution fusion | flops 38730203136 | bytes 56623104 | tf_op jit(solution)/shard_map/dot_general | solution.py:79
  936.0 108.3 %reduce-scatter.11.cloned.1.call-done = f32[768,768]{1,0:T(8,128)} async-done(((f32[6144,768]{1,0:T(8,128)}), f32[768,768]{1,0:T(8,128)}) %reduce-scatter.11.cloned.1.call-update) | async-done | bytes 2359312 | tf_op jit(solution)/shard_map/reduce_scatter | solution.py:137
  1049.5 140.1 %reduce-scatter.9.cloned.1.call-done.grad_ref = f32[384,1536]{1,0:T(8,128)} async-done(((f32[3072,1536]{1,0:T(8,128)}), f32[384,1536]{1,0:T(8,128)}) %reduce-scatter.9.cloned.1.call-update) | async-done | bytes 2359312 | tf_op jit(solution)/shard_map/reduce_scatter | solution.py:137
  1212.9 8.1 adam.4
  1236.9 8.1 adam.7
  1280.3 20.6 %collective-permute-done.46 = bf16[384,1536]{1,0:T(8,128)(2,1)} collective-permute-done((bf16[384,1536]{1,0:T(8,128)(2,1)}, bf16[384,1536]{1,0:T(8,128)(2,1)}, u32[]{:S(2)}, u32[]{:S(2)}) %collective-permute-start.46) | collective-permute-done | bytes 1179680 | tf_op jit(solution)/shard_map/ppermute | solution.py:59
  1300.8 24.7 %collective-permute-done.40 = bf16[384,1536]{1,0:T(8,128)(2,1)S(1)} collective-permute-done((bf16[384,1536]{1,0:T(8,128)(2,1)}, bf16[384,1536]{1,0:T(8,128)(2,1)S(1)}, u32[]{:S(2)}, u32[]{:S(2)}) %collective-permute-start.40) | collective-permute-done | bytes 1179680 | tf_op jit(solution)/shard_map/ppermute | solution.py:59
  (194 shorter events, 236.3 us)
Async XLA Ops:
  7.2 904.4 %reduce-scatter.7.cloned.1.call-start = ((), (), s32[]{:S(2)}) async-start(), calls=%async_computation.5 | async-start | bytes 21233664 | tf_op jit(solution)/shard_map/reduce_scatter | solution.py:137
  16.8 58.5 %collective-permute-start.2 = (bf16[384,1536]{0,1:T(8,128)(2,1)}, bf16[384,1536]{0,1:T(8,128)(2,1)}, u32[]{:S(2)}, u32[]{:S(2)}) collective-permute-start(bf16[384,1536]{0,1:T(8,128)(2,1)} %get-tuple-element.82), channel_id=1, source_target_pairs={{0,4},{4,0},{1,5},{5,1},{2,6},{6,2},{3,7},{7,3},{8,12},{12,8},{9,1... | collective-permute-start | bytes 3538952 | tf_op jit(solution)/shard_map/ppermute | solution.py:59
  18.4 50.9 %collective-permute-start.1 = (bf16[384,1536]{0,1:T(8,128)(2,1)}, bf16[384,1536]{0,1:T(8,128)(2,1)}, u32[]{:S(2)}, u32[]{:S(2)}) collective-permute-start(bf16[384,1536]{0,1:T(8,128)(2,1)} %get-tuple-element.81), channel_id=1, source_target_pairs={{0,8},{8,0},{1,9},{9,1},{2,10},{10,2},{3,11},{11,3},{4,12},{12,4},... | collective-permute-start | bytes 3538952 | tf_op jit(solution)/shard_map/ppermute | solution.py:59
  18.8 59.2 %collective-permute-start.3 = (bf16[384,1536]{0,1:T(8,128)(2,1)}, bf16[384,1536]{0,1:T(8,128)(2,1)}, u32[]{:S(2)}, u32[]{:S(2)}) collective-permute-start(bf16[384,1536]{0,1:T(8,128)(2,1)} %get-tuple-element.81), channel_id=1, source_target_pairs={{0,4},{4,0},{1,5},{5,1},{2,6},{6,2},{3,7},{7,3},{8,12},{12,8},{9,1... | collective-permute-start | bytes 3538952 | tf_op jit(solution)/shard_map/ppermute | solution.py:59
  24.7 152.4 %collective-permute-start.12 = (bf16[2048,1536]{1,0:T(8,128)(2,1)}, bf16[2048,1536]{1,0:T(8,128)(2,1)}, u32[]{:S(2)}, u32[]{:S(2)}) collective-permute-start(bf16[2048,1536]{1,0:T(8,128)(2,1)} %constant_dynamic-slice_fusion.3), channel_id=1, source_target_pairs={{0,1},{1,0},{2,3},{3,2},{4,5},{5,4},{6,7},{7,6},{8,9},{9,8},{10,11... | collective-permute-start | bytes 18874376 | tf_op jit(solution)/shard_map/ppermute | solution.py:59
  43.9 50.7 %collective-permute-start.6 = (bf16[384,1536]{1,0:T(8,128)(2,1)}, bf16[384,1536]{1,0:T(8,128)(2,1)}, u32[]{:S(2)}, u32[]{:S(2)}) collective-permute-start(bf16[384,1536]{1,0:T(8,128)(2,1)} %get-tuple-element.80), channel_id=1, source_target_pairs={{0,8},{8,0},{1,9},{9,1},{2,10},{10,2},{3,11},{11,3},{4,12},{12,4},... | collective-permute-start | bytes 3538952 | tf_op jit(solution)/shard_map/ppermute | solution.py:59
  69.3 49.7 %collective-permute-start.7 = (bf16[384,1536]{1,0:T(8,128)(2,1)}, bf16[384,1536]{1,0:T(8,128)(2,1)}, u32[]{:S(2)}, u32[]{:S(2)}) collective-permute-start(bf16[384,1536]{1,0:T(8,128)(2,1)} %get-tuple-element.79), channel_id=1, source_target_pairs={{0,8},{8,0},{1,9},{9,1},{2,10},{10,2},{3,11},{11,3},{4,12},{12,4},... | collective-permute-start | bytes 3538952 | tf_op jit(solution)/shard_map/ppermute | solution.py:59
  78.0 51.7 %collective-permute-start.9 = (bf16[384,1536]{1,0:T(8,128)(2,1)}, bf16[384,1536]{1,0:T(8,128)(2,1)S(1)}, u32[]{:S(2)}, u32[]{:S(2)}) collective-permute-start(bf16[384,1536]{1,0:T(8,128)(2,1)} %get-tuple-element.79), channel_id=1, source_target_pairs={{0,4},{4,0},{1,5},{5,1},{2,6},{6,2},{3,7},{7,3},{8,12},{12,8},{9,1... | collective-permute-start | bytes 3538952 | tf_op jit(solution)/shard_map/ppermute | solution.py:59
  94.5 60.4 %collective-permute-start.4 = (bf16[384,1536]{0,1:T(8,128)(2,1)S(1)}, bf16[384,1536]{0,1:T(8,128)(2,1)S(1)}, u32[]{:S(2)}, u32[]{:S(2)}) collective-permute-start(bf16[384,1536]{0,1:T(8,128)(2,1)S(1)} %collective-permute-done), channel_id=1, source_target_pairs={{0,4},{4,0},{1,5},{5,1},{2,6},{6,2},{3,7},{7,3},{8,12},{12,8},{9,1... | collective-permute-start | bytes 3538952 | tf_op jit(solution)/shard_map/ppermute | solution.py:59
  122.1 54.7 %collective-permute-start.10 = (bf16[384,1536]{1,0:T(8,128)(2,1)}, bf16[384,1536]{1,0:T(8,128)(2,1)S(1)}, u32[]{:S(2)}, u32[]{:S(2)}) collective-permute-start(bf16[384,1536]{1,0:T(8,128)(2,1)} %collective-permute-done.6), channel_id=1, source_target_pairs={{0,4},{4,0},{1,5},{5,1},{2,6},{6,2},{3,7},{7,3},{8,12},{12,8},{9,1... | collective-permute-start | bytes 3538952 | tf_op jit(solution)/shard_map/ppermute | solution.py:59
  237.7 63.2 %collective-permute-start.13 = (f32[2048,1536]{1,0:T(8,128)}, f32[2048,1536]{1,0:T(8,128)S(1)}, u32[]{:S(2)}, u32[]{:S(2)}) collective-permute-start(f32[2048,1536]{1,0:T(8,128)} %fusion.72), channel_id=1, source_target_pairs={{0,1},{1,0},{2,3},{3,2},{4,5},{5,4},{6,7},{7,6},{8,9},{9,8},{10,11... | collective-permute-start | bytes 37748744 | tf_op jit(solution)/shard_map/ppermute | solution.py:59
  239.3 77.5 %collective-permute-start.15 = (bf16[384,1536]{0,1:T(8,128)(2,1)}, bf16[384,1536]{0,1:T(8,128)(2,1)S(1)}, u32[]{:S(2)}, u32[]{:S(2)}) collective-permute-start(bf16[384,1536]{0,1:T(8,128)(2,1)} %get-tuple-element.84), channel_id=1, source_target_pairs={{0,8},{8,0},{1,9},{9,1},{2,10},{10,2},{3,11},{11,3},{4,12},{12,4},... | collective-permute-start | bytes 3538952 | tf_op jit(solution)/shard_map/ppermute | solution.py:59
  239.9 84.9 %collective-permute-start.17 = (bf16[384,1536]{0,1:T(8,128)(2,1)}, bf16[384,1536]{0,1:T(8,128)(2,1)}, u32[]{:S(2)}, u32[]{:S(2)}) collective-permute-start(bf16[384,1536]{0,1:T(8,128)(2,1)} %get-tuple-element.84), channel_id=1, source_target_pairs={{0,4},{4,0},{1,5},{5,1},{2,6},{6,2},{3,7},{7,3},{8,12},{12,8},{9,1... | collective-permute-start | bytes 3538952 | tf_op jit(solution)/shard_map/ppermute | solution.py:59
  241.3 76.1 %collective-permute-start.16 = (bf16[384,1536]{0,1:T(8,128)(2,1)}, bf16[384,1536]{0,1:T(8,128)(2,1)}, u32[]{:S(2)}, u32[]{:S(2)}) collective-permute-start(bf16[384,1536]{0,1:T(8,128)(2,1)} %get-tuple-element.83), channel_id=1, source_target_pairs={{0,8},{8,0},{1,9},{9,1},{2,10},{10,2},{3,11},{11,3},{4,12},{12,4},... | collective-permute-start | bytes 3538952 | tf_op jit(solution)/shard_map/ppermute | solution.py:59
  242.9 84.5 %collective-permute-start.18 = (bf16[384,1536]{0,1:T(8,128)(2,1)}, bf16[384,1536]{0,1:T(8,128)(2,1)}, u32[]{:S(2)}, u32[]{:S(2)}) collective-permute-start(bf16[384,1536]{0,1:T(8,128)(2,1)} %get-tuple-element.83), channel_id=1, source_target_pairs={{0,4},{4,0},{1,5},{5,1},{2,6},{6,2},{3,7},{7,3},{8,12},{12,8},{9,1... | collective-permute-start | bytes 3538952 | tf_op jit(solution)/shard_map/ppermute | solution.py:59
  305.8 125.1 %collective-permute-start.14 = (bf16[2048,1536]{1,0:T(8,128)(2,1)}, bf16[2048,1536]{1,0:T(8,128)(2,1)}, u32[]{:S(2)}, u32[]{:S(2)}) collective-permute-start(bf16[2048,1536]{1,0:T(8,128)(2,1)} %add_convert_fusion.1), channel_id=1, source_target_pairs={{0,1},{1,0},{2,3},{3,2},{4,5},{5,4},{6,7},{7,6},{8,9},{9,8},{10,11... | collective-permute-start | bytes 18874376 | tf_op jit(solution)/shard_map/ppermute | solution.py:59
  317.4 53.4 %collective-permute-start.23 = (bf16[384,1536]{1,0:T(8,128)(2,1)}, bf16[384,1536]{1,0:T(8,128)(2,1)}, u32[]{:S(2)}, u32[]{:S(2)}) collective-permute-start(bf16[384,1536]{1,0:T(8,128)(2,1)} %get-tuple-element.77), channel_id=1, source_target_pairs={{0,8},{8,0},{1,9},{9,1},{2,10},{10,2},{3,11},{11,3},{4,12},{12,4},... | collective-permute-start | bytes 3538952 | tf_op jit(solution)/shard_map/ppermute | solution.py:59
  327.4 51.7 %collective-permute-start.25 = (bf16[384,1536]{1,0:T(8,128)(2,1)}, bf16[384,1536]{1,0:T(8,128)(2,1)S(1)}, u32[]{:S(2)}, u32[]{:S(2)}) collective-permute-start(bf16[384,1536]{1,0:T(8,128)(2,1)} %get-tuple-element.77), channel_id=1, source_target_pairs={{0,4},{4,0},{1,5},{5,1},{2,6},{6,2},{3,7},{7,3},{8,12},{12,8},{9,1... | collective-permute-start | bytes 3538952 | tf_op jit(solution)/shard_map/ppermute | solution.py:59
  346.0 58.4 %collective-permute-start.19 = (bf16[384,1536]{0,1:T(8,128)(2,1)S(1)}, bf16[384,1536]{0,1:T(8,128)(2,1)S(1)}, u32[]{:S(2)}, u32[]{:S(2)}) collective-permute-start(bf16[384,1536]{0,1:T(8,128)(2,1)S(1)} %collective-permute-done.15), channel_id=1, source_target_pairs={{0,4},{4,0},{1,5},{5,1},{2,6},{6,2},{3,7},{7,3},{8,12},{12,8},{9,1... | collective-permute-start | bytes 3538952 | tf_op jit(solution)/shard_map/ppermute | solution.py:59
  373.8 54.9 %collective-permute-start.26 = (bf16[384,1536]{1,0:T(8,128)(2,1)}, bf16[384,1536]{1,0:T(8,128)(2,1)S(1)}, u32[]{:S(2)}, u32[]{:S(2)}) collective-permute-start(bf16[384,1536]{1,0:T(8,128)(2,1)} %collective-permute-done.22), channel_id=1, source_target_pairs={{0,4},{4,0},{1,5},{5,1},{2,6},{6,2},{3,7},{7,3},{8,12},{12,8},{9,1... | collective-permute-start | bytes 3538952 | tf_op jit(solution)/shard_map/ppermute | solution.py:59
  379.1 50.7 %collective-permute-start.27 = (bf16[384,1536]{1,0:T(8,128)(2,1)S(1)}, bf16[384,1536]{1,0:T(8,128)(2,1)S(1)}, u32[]{:S(2)}, u32[]{:S(2)}) collective-permute-start(bf16[384,1536]{1,0:T(8,128)(2,1)S(1)} %collective-permute-done.25), channel_id=1, source_target_pairs={{0,8},{8,0},{1,9},{9,1},{2,10},{10,2},{3,11},{11,3},{4,12},{12,4},... | collective-permute-start | bytes 3538952 | tf_op jit(solution)/shard_map/ppermute | solution.py:59
  404.4 71.2 %collective-permute-start.21 = (bf16[2048,1536]{1,0:T(8,128)(2,1)S(1)}, bf16[2048,1536]{1,0:T(8,128)(2,1)}, u32[]{:S(2)}, u32[]{:S(2)}) collective-permute-start(bf16[2048,1536]{1,0:T(8,128)(2,1)S(1)} %copy-done.7), channel_id=1, source_target_pairs={{0,1},{1,0},{2,3},{3,2},{4,5},{5,4},{6,7},{7,6},{8,9},{9,8},{10,11... | collective-permute-start | bytes 18874376 | tf_op jit(solution)/shard_map/ppermute | solution.py:59
  612.1 310.4 %reduce-scatter.5.cloned.1.call-start = ((), (), s32[]{:S(2)}) async-start(), calls=%async_computation.4 | async-start | bytes 21233664 | tf_op jit(solution)/shard_map/reduce_scatter | solution.py:137
  638.8 81.9 %collective-permute-start.28 = (f32[2048,1536]{1,0:T(8,128)}, f32[2048,1536]{1,0:T(8,128)}, u32[]{:S(2)}, u32[]{:S(2)}) collective-permute-start(f32[2048,1536]{1,0:T(8,128)} %fusion.41), channel_id=1, source_target_pairs={{0,1},{1,0},{2,3},{3,2},{4,5},{5,4},{6,7},{7,6},{8,9},{9,8},{10,11... | collective-permute-start | bytes 37748744 | tf_op jit(solution)/shard_map/ppermute | solution.py:59
  695.6 348.7 %reduce-scatter.11.cloned.1.call-start = ((), (), s32[]{:S(2)}) async-start(), calls=%async_computation.7 | async-start | bytes 21233664 | tf_op jit(solution)/shard_map/reduce_scatter | solution.py:137
  860.3 329.3 %reduce-scatter.9.cloned.1.call-start = ((), (), s32[]{:S(2)}) async-start(), calls=%async_computation.6 | async-start | bytes 21233664 | tf_op jit(solution)/shard_map/reduce_scatter | solution.py:137
  1049.5 200.9 %collective-permute-start.38 = (f32[384,2,384]{2,1,0:T(2,128)}, f32[384,2,384]{2,1,0:T(2,128)S(1)}, u32[]{:S(2)}, u32[]{:S(2)}) collective-permute-start(f32[384,2,384]{2,1,0:T(2,128)} %get-tuple-element.74), channel_id=1, source_target_pairs={{0,1},{1,0},{2,3},{3,2},{4,5},{5,4},{6,7},{7,6},{8,9},{9,8},{10,11... | collective-permute-start | bytes 3538952 | tf_op jit(solution)/shard_map/ppermute | solution.py:59
  1250.4 50.4 %collective-permute-start.46 = (bf16[384,1536]{1,0:T(8,128)(2,1)}, bf16[384,1536]{1,0:T(8,128)(2,1)}, u32[]{:S(2)}, u32[]{:S(2)}) collective-permute-start(bf16[384,1536]{1,0:T(8,128)(2,1)} %get-tuple-element.58), channel_id=1, source_target_pairs={{0,2},{2,0},{1,3},{3,1},{4,6},{6,4},{5,7},{7,5},{8,10},{10,8},{9,1... | collective-permute-start | bytes 3538952 | tf_op jit(solution)/shard_map/ppermute | solution.py:59
  1267.4 58.1 %collective-permute-start.40 = (bf16[384,1536]{1,0:T(8,128)(2,1)}, bf16[384,1536]{1,0:T(8,128)(2,1)S(1)}, u32[]{:S(2)}, u32[]{:S(2)}) collective-permute-start(bf16[384,1536]{1,0:T(8,128)(2,1)} %get-tuple-element.53), channel_id=1, source_target_pairs={{0,2},{2,0},{1,3},{3,1},{4,6},{6,4},{5,7},{7,5},{8,10},{10,8},{9,1... | collective-permute-start | bytes 3538952 | tf_op jit(solution)/shard_map/ppermute | solution.py:59
  1268.0 57.5 %collective-permute-start.37 = (bf16[384,1536]{1,0:T(8,128)(2,1)}, bf16[384,1536]{1,0:T(8,128)(2,1)S(1)}, u32[]{:S(2)}, u32[]{:S(2)}) collective-permute-start(bf16[384,1536]{1,0:T(8,128)(2,1)} %collective-permute-done.36), channel_id=1, source_target_pairs={{0,1},{1,0},{2,3},{3,2},{4,5},{5,4},{6,7},{7,6},{8,9},{9,8},{10,11... | collective-permute-start | bytes 3538952 | tf_op jit(solution)/shard_map/ppermute | solution.py:59
  1272.7 61.1 %collective-permute-start.45 = (bf16[384,1536]{1,0:T(8,128)(2,1)}, bf16[384,1536]{1,0:T(8,128)(2,1)S(1)}, u32[]{:S(2)}, u32[]{:S(2)}) collective-permute-start(bf16[384,1536]{1,0:T(8,128)(2,1)} %get-tuple-element.58), channel_id=1, source_target_pairs={{0,1},{1,0},{2,3},{3,2},{4,5},{5,4},{6,7},{7,6},{8,9},{9,8},{10,11... | collective-permute-start | bytes 3538952 | tf_op jit(solution)/shard_map/ppermute | solution.py:59
  1275.5 52.6 %collective-permute-start.44 = (bf16[384,1536]{1,0:T(8,128)(2,1)}, bf16[384,1536]{1,0:T(8,128)(2,1)S(1)}, u32[]{:S(2)}, u32[]{:S(2)}) collective-permute-start(bf16[384,1536]{1,0:T(8,128)(2,1)} %collective-permute-done.43), channel_id=1, source_target_pairs={{0,1},{1,0},{2,3},{3,2},{4,5},{5,4},{6,7},{7,6},{8,9},{9,8},{10,11... | collective-permute-start | bytes 3538952 | tf_op jit(solution)/shard_map/ppermute | solution.py:59
  (32 other events, 909.1 us)
Sparse Core Ops, SparseCore 0:
  612.3 141.0 reduce-scatter.6
  757.7 141.0 reduce-scatter.4
  903.2 141.0 reduce-scatter.10
  1048.5 141.0 reduce-scatter.8

commit v2 on v1

--- a/solution.py
+++ b/solution.py
@@ -1,3 +1,5 @@
+import math
+
 import jax
 import jax.numpy as jnp
 from jax import lax
@@ -12,6 +14,9 @@
 ADAM_EPS = 1e-8
 NORM_EPS = 1e-6
 DATA = 4
+AXES = ("z", "y", "x", "c")
+GELU_A = (2.0 / math.pi) ** 0.5
+GELU_B = 0.044715 * GELU_A
 
 
 def gelu_fwd(z_low):
@@ -19,8 +24,55 @@
 
 
 def gelu_back(z_low, grad_low):
-    _, back_fn = jax.vjp(jax.nn.gelu, z_low.astype(jnp.float32))
-    return back_fn(grad_low.astype(jnp.float32))[0].astype(jnp.bfloat16)
+    z, grad = z_low.astype(jnp.float32), grad_low.astype(jnp.float32)
+    square = z * z
+    tanh = jnp.tanh(z * (GELU_A + GELU_B * square))
+    slope = (0.5 + 0.5 * tanh) + z * (1.0 - tanh * tanh) * (0.5 * GELU_A + 1.5 * GELU_B * square)
+    return (grad * slope).astype(jnp.bfloat16)
+
+
+def norm_kernel(part_ref, total_ref, held, send_sem, recv_sem):
+    here = [lax.axis_index(axis) for axis in AXES]
+    place = lambda spot: 8 * spot[0] + 4 * spot[1] + 2 * spot[2] + spot[3]
+    peers = [[1 - pos if step >> (3 - i) & 1 else pos for i, pos in enumerate(here)] for step in range(1, 16)]
+    barrier = pltpu.get_barrier_semaphore()
+    for peer in peers:
+        pl.semaphore_signal(barrier, inc=1, device_id=tuple(peer), device_id_type=pl.DeviceIdType.MESH)
+    pl.semaphore_wait(barrier, 15)
+    held[place(here)] = part_ref[...]
+
+    def copy(step, peer, slot):
+        return pltpu.make_async_remote_copy(
+            src_ref=part_ref,
+            dst_ref=held.at[slot],
+            send_sem=send_sem.at[step],
+            recv_sem=recv_sem.at[slot],
+            device_id=tuple(peer),
+            device_id_type=pl.DeviceIdType.MESH,
+        )
+
+    for step, peer in enumerate(peers):
+        copy(step, peer, place(here)).start()
+    for step, peer in enumerate(peers):
+        copy(step, peer, place(here)).wait_send()
+        copy(step, peer, place(peer)).wait_recv()
+    total = held[0]
+    for slot in range(1, 16):
+        total = total + held[slot]
+    total_ref[...] = total
+
+
+def norm_sum(part):
+    vmem = pl.BlockSpec(memory_space=pltpu.VMEM)
+    return pl.pallas_call(
+        norm_kernel,
+        out_shape=jax.ShapeDtypeStruct((8, 128), jnp.float32),
+        in_specs=[vmem],
+        out_specs=vmem,
+        scratch_shapes=[pltpu.VMEM((16, 8, 128), jnp.float32), pltpu.SemaphoreType.DMA((15,)), pltpu.SemaphoreType.DMA((16,))],
+        compiler_params=pltpu.CompilerParams(collective_id=0, has_side_effects=True),
+        name="norm",
+    )(jnp.broadcast_to(part, (8, 128)))[0, :1]
 
 
 def adam_kernel(scale_ref, lr_ref, master_ref, mom_ref, var_ref, grad_ref, *refs):
@@ -117,13 +169,15 @@
         x_all = jnp.concatenate([x_own, x_oth], 0)
         dy_all = jnp.concatenate([dy_own, dy_oth], 0)
         w_two = gather_model(down_block(0))
-        w_three = gather_model(up_block(1))
-        w_four = gather_model(down_block(1))
 
         z_one_oth = dot(x_oth, w_one, ((1,), (1,))).astype(jnp.bfloat16)
         act_one_oth = gelu_fwd(z_one_oth)
         z_one_own = dot(x_own, w_one, ((1,), (1,))).astype(jnp.bfloat16)
         act_one_own = gelu_fwd(z_one_own)
+        share = lambda block: lax.dynamic_slice_in_dim(block, x_pos * piece, piece, 0)
+        share_three, share_four, z_one_own, act_one_own = lax.optimization_barrier((share(up_block(1)), share(down_block(1)), z_one_own, act_one_own))
+        w_three = lax.all_gather(share_three, ("z", "y", "x"), axis=0, tiled=True)
+        w_four = lax.all_gather(share_four, ("z", "y", "x"), axis=0, tiled=True)
         hid_oth = dot(act_one_oth, w_two, ((1,), (0,)))
         hid_own = dot(act_one_own, w_two, ((1,), (0,)))
         z_one = jnp.concatenate([z_one_own, z_one_oth], 0)
@@ -140,12 +194,12 @@
             return grad.reshape(dim, 4, 2 * piece).transpose(1, 0, 2).reshape(4 * dim, 2 * piece)
 
         def core_exchange(mine):
-            mine = mine.reshape(2, piece, 2, piece)
-            keep = lax.dynamic_index_in_dim(mine, core, 0, keepdims=False)
-            give = lax.dynamic_index_in_dim(mine, 1 - core, 0, keepdims=False)
+            mine, core = lax.optimization_barrier((mine, lax.axis_index("c")))
+            keep = lax.dynamic_slice_in_dim(mine, core * piece, piece, 0)
+            give = lax.dynamic_slice_in_dim(mine, (1 - core) * piece, piece, 0)
             got = swap(give, "c")
-            pair = jnp.where(core == 0, jnp.stack([keep, got], 2), jnp.stack([got, keep], 2))
-            return pair.reshape(piece, dim)
+            low, high = jnp.where(core == 0, keep, got), jnp.where(core == 0, got, keep)
+            return jnp.concatenate([low[:, :piece], high[:, :piece], low[:, piece:], high[:, piece:]], 1)
 
         grad_w4 = dot(act_two, dy_all, ((0,), (0,)))
         sum_w4 = scatter(grad_w4)
@@ -167,8 +221,7 @@
         total = jnp.zeros((1,), jnp.float32)
         for part in (sum_w4, sum_w3, sum_w2, sum_w1):
             total = total + jnp.sum((part / DATA) * (part / DATA))
-        for axis in ("c", "x", "y", "z"):
-            total = total + swap(total, axis)
+        total = norm_sum(total)
         norm_val = jnp.sqrt(total)
         clip_scale = jnp.minimum(1.0, clip_norm[0] / (norm_val[0] + NORM_EPS))
         sum_w1, sum_w3 = core_exchange(sum_w1), core_exchange(sum_w3)

time: 1350 us -> 1210 us (0.90)
  waiting for transfers between devices: 492 us -> 407 us
  local copies, waits for them, and re-layouts: 142 us -> 110 us
  starting transfers between devices: 44.2 us -> 25.9 us
    ppermute x48 -> x32, waiting for transfers between devices: 244 us -> 141 us  [swap(): return lax.ppermute(arr, axis, [(0, 1), (1, 0)])]
    ppermute x48 -> x32, starting transfers between devices: 44.1 us -> 25 us  [swap(): return lax.ppermute(arr, axis, [(0, 1), (1, 0)])]
  transfers between devices with their start and end apart: 52 -> 38, of which waited for: 20 -> 13; matrix products, arithmetic and copies ran while one was open for 41% -> 47% of each run, Pallas kernels for 2% -> 2%
where the time goes in v2:
time: 1210 us; the launch traced here: 1200 us
  matrix products  539 us (45%)
  waiting for transfers between devices  407 us (34%)
  local copies, waits for them, and re-layouts  110 us (9%)
  other arithmetic  57.6 us (5%)
  Pallas kernels  39.8 us (3%)
  starting transfers between devices  25.9 us (2%)
  between operations  20.6 us (2%)
    dot_general x13, matrix products, dot(): lax.dot_general(left, right, (dims, ((), ())), preferred_element_type=jnp...  539 us
    reduce_scatter x4, waiting for transfers between devices, scatter(): lax.psum_scatter(grad, ('z', 'y', 'x'), scatter_dimension=0, tiled=True)  253 us
    ppermute x32, waiting for transfers between devices, swap(): return lax.ppermute(arr, axis, [(0, 1), (1, 0)])  141 us
    pallas_call x4, Pallas kernels, adam_update(): pl.pallas_call(adam_kernel, grid=(6,), out_shape=[jax.ShapeDtypeStruct(ma...  32.4 us
    reshape x2, local copies, waits for them, and re-layouts, model_major(): grad.reshape(dim, 4, 2 * piece).transpose(1, 0, 2)  29.4 us
    ppermute x32, starting transfers between devices, swap(): return lax.ppermute(arr, axis, [(0, 1), (1, 0)])  25 us
  transfers between devices with their start and end apart: 38, of which 13 were waited for; matrix products, arithmetic and copies ran while one was open for 47% of the time, Pallas kernels for 2%

profile of v2, /device:TPU:0, one launch (start us, length us, event | category | flops | bytes accessed | tf_op | source)
XLA Modules:
  0.0 1200.0 jit_solution(15512999988474506065)
XLA Ops:
  50.2 17.6 %collective-permute-done.1 = bf16[384,1536]{0,1:T(8,128)(2,1)} collective-permute-done((bf16[384,1536]{0,1:T(8,128)(2,1)}, bf16[384,1536]{0,1:T(8,128)(2,1)}, u32[]{:S(2)}, u32[]{:S(2)}) %collective-permute-start.1) | collective-permute-done | bytes 1179680 | tf_op jit(solution)/shard_map/ppermute | solution.py:111
  79.0 14.1 %collective-permute-done.6 = bf16[384,1536]{1,0:T(8,128)(2,1)} collective-permute-done((bf16[384,1536]{1,0:T(8,128)(2,1)}, bf16[384,1536]{1,0:T(8,128)(2,1)}, u32[]{:S(2)}, u32[]{:S(2)}) %collective-permute-start.6) | collective-permute-done | bytes 1179680 | tf_op jit(solution)/shard_map/ppermute | solution.py:111
  93.1 24.3 %collective-permute-done.7 = bf16[384,1536]{1,0:T(8,128)(2,1)S(1)} collective-permute-done((bf16[384,1536]{1,0:T(8,128)(2,1)}, bf16[384,1536]{1,0:T(8,128)(2,1)S(1)}, u32[]{:S(2)}, u32[]{:S(2)}) %collective-permute-start.7) | collective-permute-done | bytes 1179680 | tf_op jit(solution)/shard_map/ppermute | solution.py:111
  126.8 20.7 %collective-permute-done.4 = bf16[384,1536]{0,1:T(8,128)(2,1)S(1)} collective-permute-done((bf16[384,1536]{0,1:T(8,128)(2,1)}, bf16[384,1536]{0,1:T(8,128)(2,1)S(1)}, u32[]{:S(2)}, u32[]{:S(2)}) %collective-permute-start.4) | collective-permute-done | bytes 1179680 | tf_op jit(solution)/shard_map/ppermute | solution.py:111
  148.1 35.2 %fusion.29 = (bf16[2048,3072]{1,0:T(8,128)(2,1)}, bf16[2048,3072]{1,0:T(8,128)(2,1)}) fusion(bf16[2048,1536]{1,0:T(8,128)(2,1)} %constant_dynamic-slice_fusion.3, bf16[3072,1536]{0,1:T(8,128)(2,1)S(1)} %constant_dynamic-update-slice_fusion.6), kind=kOutput, calls=%fused_computation.46 | convolution fusion | flops 19396558848 | bytes 40894464 | tf_op jit(solution)/shard_map/dot_general | solution.py:131
  185.9 33.2 %fusion.35 = (bf16[2048,3072]{1,0:T(8,128)(2,1)}, bf16[2048,3072]{1,0:T(8,128)(2,1)}) fusion(bf16[2048,1536]{1,0:T(8,128)(2,1)} %collective-permute-done.12, bf16[3072,1536]{0,1:T(8,128)(2,1)} %copy-done.3), kind=kOutput, calls=%fused_computation.52 | convolution fusion | flops 19396558848 | bytes 40894464 | tf_op jit(solution)/shard_map/dot_general | solution.py:131
  219.1 24.0 %fusion.79 = f32[2048,1536]{1,0:T(8,128)} fusion(bf16[2048,3072]{1,0:T(8,128)(2,1)} %get-tuple-element.95, bf16[3072,1536]{1,0:T(8,128)(2,1)S(1)} %copy-done.1), kind=kOutput, calls=%fused_computation.162 | convolution fusion | flops 19327352832 | bytes 34603008 | tf_op jit(solution)/shard_map/dot_general | solution.py:131
  243.6 24.3 %fusion.78 = f32[2048,1536]{1,0:T(8,128)S(1)} fusion(bf16[2048,3072]{1,0:T(8,128)(2,1)} %get-tuple-element.42, bf16[3072,1536]{1,0:T(8,128)(2,1)} %constant_dynamic-update-slice_fusion), kind=kOutput, calls=%fused_computation.161 | convolution fusion | flops 19327352832 | bytes 34603008 | tf_op jit(solution)/shard_map/dot_general | solution.py:131
  268.0 9.2 add_convert_fusion.1
  287.8 47.5 %convolution_convert_fusion = bf16[4096,3072]{1,0:T(8,128)(2,1)} fusion(bf16[3072,1536]{0,1:T(8,128)(2,1)} %all-gather.3.cloned.1.call-done, bf16[2048,1536]{1,0:T(8,128)(2,1)} %collective-permute-done.14, bf16[2048,1536]{1,0:T(8,128)(2,1)} %add_convert_fusion.1), kind=kOutput, calls=%fused_computation.59 | convolution fusion | flops 38692454400 | bytes 47185920 | tf_op jit(solution)/shard_map/dot_general | solution.py:131
  335.4 13.1 %all-gather.5.cloned.1.call-done = bf16[3072,1536]{1,0:T(8,128)(2,1)} async-done(((bf16[384,1536]{1,0:T(8,128)(2,1)}), bf16[3072,1536]{1,0:T(8,128)(2,1)}) %all-gather.5.cloned.1.call-update) | async-done | bytes 9437200 | tf_op jit(solution)/shard_map/all_gather | solution.py:180
  348.5 64.8 %fusion.16 = bf16[4096,3072]{1,0:T(8,128)(2,1)} fusion(bf16[4096,3072]{1,0:T(8,128)(2,1)} %convolution_convert_fusion, bf16[3072,1536]{1,0:T(8,128)(2,1)} %all-gather.5.cloned.1.call-done, bf16[2048,1536]{1,0:T(8,128)(2,1)} %collective-permute-done.15, bf16[2048,1536]{1,0:T(8,128)(2,1)} %constant_dynamic-slice_fusion.2), kind=kOutput, calls=%fused_computation.25 | convolution fusion | flops 38906363904 | bytes 72351744 | tf_op jit(solution)/shard_map/dot_general | solution.py:131
  413.2 49.0 %fusion.52 = f32[1536,3072]{1,0:T(8,128)} fusion(bf16[4096,3072]{1,0:T(8,128)(2,1)} %fusion.16, bf16[2048,1536]{1,0:T(8,128)(2,1)} %collective-permute-done.14, bf16[2048,1536]{1,0:T(8,128)(2,1)} %add_convert_fusion.1), kind=kOutput, calls=%fused_computation.79 | convolution fusion | flops 38679871488 | bytes 56623104 | tf_op jit(solution)/shard_map/dot_general | solution.py:131
  462.2 14.5 %copy.34 = f32[192,4,8,768]{3,2,0,1:T(8,128)} copy(f32[192,4,8,768]{3,2,1,0:T(8,128)} %bitcast.90) | data formatting | bytes 37748736 | tf_op jit(solution)/shard_map/reshape | solution.py:194
  476.9 56.5 %fusion.40 = f32[3072,1536]{1,0:T(8,128)} fusion(bf16[4096,3072]{1,0:T(8,128)(2,1)} %convolution_convert_fusion, bf16[2048,1536]{1,0:T(8,128)(2,1)} %collective-permute-done.15, bf16[2048,1536]{1,0:T(8,128)(2,1)} %constant_dynamic-slice_fusion.2), kind=kOutput, calls=%fused_computation.57 | convolution fusion | flops 38805700608 | bytes 56623104 | tf_op jit(solution)/shard_map/dot_general | solution.py:131
  533.4 27.7 %fusion.44 = f32[2048,1536]{1,0:T(8,128)} fusion(bf16[3072,1536]{0,1:T(8,128)(2,1)} %all-gather.3.cloned.1.call-done, bf16[4096,3072]{1,0:T(8,128)(2,1)} %fusion.16), kind=kOutput, calls=%fused_computation.62 | convolution fusion | flops 19327352832 | bytes 34603008 | tf_op jit(solution)/shard_map/dot_general | solution.py:131
  561.1 27.3 %fusion.46 = f32[2048,1536]{1,0:T(8,128)} fusion(bf16[3072,1536]{0,1:T(8,128)(2,1)} %all-gather.3.cloned.1.call-done, bf16[4096,3072]{1,0:T(8,128)(2,1)} %fusion.16), kind=kOutput, calls=%fused_computation.64 | convolution fusion | flops 19327352832 | bytes 34603008 | tf_op jit(solution)/shard_map/dot_general | solution.py:131
  597.7 9.9 collective-permute-done.17
  607.7 50.5 %fusion.36 = f32[3072,1536]{1,0:T(8,128)} fusion(bf16[2048,3072]{1,0:T(8,128)(2,1)} %get-tuple-element.95, bf16[2048,3072]{1,0:T(8,128)(2,1)} %get-tuple-element.42, bf16[2048,1536]{1,0:T(8,128)(2,1)} %collective-permute-done.17, bf16[2048,1536]{1,0:T(8,128)(2,1)} %copy-done.5), kind=kOutput, calls=%fused_computation.53 | convolution fusion | flops 38730203136 | bytes 56623104 | tf_op jit(solution)/shard_map/dot_general | solution.py:131
  658.3 11.2 fusion.107
  669.5 47.5 %fusion.51 = bf16[4096,3072]{1,0:T(8,128)(2,1)} fusion(bf16[3072,1536]{1,0:T(8,128)(2,1)} %constant_dynamic-update-slice_fusion, bf16[2048,1536]{1,0:T(8,128)(2,1)} %collective-permute-done.17, bf16[2048,1536]{1,0:T(8,128)(2,1)} %copy-done.5), kind=kOutput, calls=%fused_computation.78 | convolution fusion | flops 38679871488 | bytes 47185920 | tf_op jit(solution)/shard_map/dot_general | solution.py:131
  716.9 51.9 %fusion.42 = f32[1536,3072]{1,0:T(8,128)} fusion(bf16[2048,3072]{1,0:T(8,128)(2,1)} %get-tuple-element.96, bf16[2048,3072]{1,0:T(8,128)(2,1)} %get-tuple-element.48, bf16[4096,3072]{1,0:T(8,128)(2,1)} %fusion.51, bf16[4096,1536]{1,0:T(8,128)(2,1)} %fusion.107), kind=kOutput, calls=%fused_computation.58 | convolution fusion | flops 38906363904 | bytes 81788928 | tf_op jit(solution)/shard_map/dot_general | solution.py:131
  768.8 14.9 %copy.33 = f32[192,4,8,768]{3,2,0,1:T(8,128)} copy(f32[192,4,8,768]{3,2,1,0:T(8,128)} %bitcast.89) | data formatting | bytes 37748736 | tf_op jit(solution)/shard_map/reshape | solution.py:194
  797.7 110.9 %reduce-scatter.9.cloned.1.call-done.grad_ref = f32[384,1536]{1,0:T(8,128)} async-done(((f32[3072,1536]{1,0:T(8,128)}), f32[384,1536]{1,0:T(8,128)}) %reduce-scatter.9.cloned.1.call-update) | async-done | bytes 2359312 | tf_op jit(solution)/shard_map/reduce_scatter | solution.py:191
  912.2 141.8 %reduce-scatter.11.cloned.1.call-done = f32[768,768]{1,0:T(8,128)} async-done(((f32[6144,768]{1,0:T(8,128)}), f32[768,768]{1,0:T(8,128)}) %reduce-scatter.11.cloned.1.call-update) | async-done | bytes 2359312 | tf_op jit(solution)/shard_map/reduce_scatter | solution.py:191
  1067.4 8.1 adam.4
  1077.0 8.1 adam.6
  1093.7 8.1 adam.7
  1113.3 8.1 adam.5
  1121.9 8.1 collective-permute-done.27
  1134.7 20.1 %collective-permute-done.30 = bf16[384,1536]{1,0:T(8,128)(2,1)} collective-permute-done((bf16[384,1536]{1,0:T(8,128)(2,1)}, bf16[384,1536]{1,0:T(8,128)(2,1)}, u32[]{:S(2)}, u32[]{:S(2)}) %collective-permute-start.30) | collective-permute-done | bytes 1179680 | tf_op jit(solution)/shard_map/ppermute | solution.py:111
  1164.3 18.1 %collective-permute-done.24 = bf16[384,1536]{1,0:T(8,128)(2,1)S(1)} collective-permute-done((bf16[384,1536]{1,0:T(8,128)(2,1)}, bf16[384,1536]{1,0:T(8,128)(2,1)S(1)}, u32[]{:S(2)}, u32[]{:S(2)}) %collective-permute-start.24) | collective-permute-done | bytes 1179680 | tf_op jit(solution)/shard_map/ppermute | solution.py:111
  (150 shorter events, 158.9 us)
Async XLA Ops:
  7.2 276.3 %all-gather.3.cloned.1.call-start = ((), (), s32[]{:S(2)}) async-start(), calls=%async_computation.4 | async-start | bytes 10616832 | tf_op jit(solution)/shard_map/all_gather | solution.py:179
  12.1 30.4 %collective-permute-start = (bf16[384,1536]{0,1:T(8,128)(2,1)}, bf16[384,1536]{0,1:T(8,128)(2,1)}, u32[]{:S(2)}, u32[]{:S(2)}) collective-permute-start(bf16[384,1536]{0,1:T(8,128)(2,1)} %get-tuple-element.84), channel_id=1, source_target_pairs={{0,8},{8,0},{1,9},{9,1},{2,10},{10,2},{3,11},{11,3},{4,12},{12,4},... | collective-permute-start | bytes 3538952 | tf_op jit(solution)/shard_map/ppermute | solution.py:111
  15.4 54.4 %collective-permute-start.2 = (bf16[384,1536]{0,1:T(8,128)(2,1)}, bf16[384,1536]{0,1:T(8,128)(2,1)}, u32[]{:S(2)}, u32[]{:S(2)}) collective-permute-start(bf16[384,1536]{0,1:T(8,128)(2,1)} %get-tuple-element.84), channel_id=1, source_target_pairs={{0,4},{4,0},{1,5},{5,1},{2,6},{6,2},{3,7},{7,3},{8,12},{12,8},{9,1... | collective-permute-start | bytes 3538952 | tf_op jit(solution)/shard_map/ppermute | solution.py:111
  16.9 50.9 %collective-permute-start.1 = (bf16[384,1536]{0,1:T(8,128)(2,1)}, bf16[384,1536]{0,1:T(8,128)(2,1)}, u32[]{:S(2)}, u32[]{:S(2)}) collective-permute-start(bf16[384,1536]{0,1:T(8,128)(2,1)} %get-tuple-element.83), channel_id=1, source_target_pairs={{0,8},{8,0},{1,9},{9,1},{2,10},{10,2},{3,11},{11,3},{4,12},{12,4},... | collective-permute-start | bytes 3538952 | tf_op jit(solution)/shard_map/ppermute | solution.py:111
  17.4 57.3 %collective-permute-start.3 = (bf16[384,1536]{0,1:T(8,128)(2,1)}, bf16[384,1536]{0,1:T(8,128)(2,1)}, u32[]{:S(2)}, u32[]{:S(2)}) collective-permute-start(bf16[384,1536]{0,1:T(8,128)(2,1)} %get-tuple-element.83), channel_id=1, source_target_pairs={{0,4},{4,0},{1,5},{5,1},{2,6},{6,2},{3,7},{7,3},{8,12},{12,8},{9,1... | collective-permute-start | bytes 3538952 | tf_op jit(solution)/shard_map/ppermute | solution.py:111
  20.5 72.6 %collective-permute-start.6 = (bf16[384,1536]{1,0:T(8,128)(2,1)}, bf16[384,1536]{1,0:T(8,128)(2,1)}, u32[]{:S(2)}, u32[]{:S(2)}) collective-permute-start(bf16[384,1536]{1,0:T(8,128)(2,1)} %get-tuple-element.82), channel_id=1, source_target_pairs={{0,8},{8,0},{1,9},{9,1},{2,10},{10,2},{3,11},{11,3},{4,12},{12,4},... | collective-permute-start | bytes 3538952 | tf_op jit(solution)/shard_map/ppermute | solution.py:111
  42.5 74.9 %collective-permute-start.7 = (bf16[384,1536]{1,0:T(8,128)(2,1)}, bf16[384,1536]{1,0:T(8,128)(2,1)S(1)}, u32[]{:S(2)}, u32[]{:S(2)}) collective-permute-start(bf16[384,1536]{1,0:T(8,128)(2,1)} %get-tuple-element.81), channel_id=1, source_target_pairs={{0,8},{8,0},{1,9},{9,1},{2,10},{10,2},{3,11},{11,3},{4,12},{12,4},... | collective-permute-start | bytes 3538952 | tf_op jit(solution)/shard_map/ppermute | solution.py:111
  67.8 54.8 %collective-permute-start.8 = (bf16[384,1536]{1,0:T(8,128)(2,1)}, bf16[384,1536]{1,0:T(8,128)(2,1)S(1)}, u32[]{:S(2)}, u32[]{:S(2)}) collective-permute-start(bf16[384,1536]{1,0:T(8,128)(2,1)} %get-tuple-element.82), channel_id=1, source_target_pairs={{0,4},{4,0},{1,5},{5,1},{2,6},{6,2},{3,7},{7,3},{8,12},{12,8},{9,1... | collective-permute-start | bytes 3538952 | tf_op jit(solution)/shard_map/ppermute | solution.py:111
  69.8 54.4 %collective-permute-start.9 = (bf16[384,1536]{1,0:T(8,128)(2,1)}, bf16[384,1536]{1,0:T(8,128)(2,1)S(1)}, u32[]{:S(2)}, u32[]{:S(2)}) collective-permute-start(bf16[384,1536]{1,0:T(8,128)(2,1)} %get-tuple-element.81), channel_id=1, source_target_pairs={{0,4},{4,0},{1,5},{5,1},{2,6},{6,2},{3,7},{7,3},{8,12},{12,8},{9,1... | collective-permute-start | bytes 3538952 | tf_op jit(solution)/shard_map/ppermute | solution.py:111
  74.6 72.8 %collective-permute-start.4 = (bf16[384,1536]{0,1:T(8,128)(2,1)}, bf16[384,1536]{0,1:T(8,128)(2,1)S(1)}, u32[]{:S(2)}, u32[]{:S(2)}) collective-permute-start(bf16[384,1536]{0,1:T(8,128)(2,1)} %collective-permute-done), channel_id=1, source_target_pairs={{0,4},{4,0},{1,5},{5,1},{2,6},{6,2},{3,7},{7,3},{8,12},{12,8},{9,1... | collective-permute-start | bytes 3538952 | tf_op jit(solution)/shard_map/ppermute | solution.py:111
  93.1 92.8 %collective-permute-start.12 = (bf16[2048,1536]{1,0:T(8,128)(2,1)}, bf16[2048,1536]{1,0:T(8,128)(2,1)}, u32[]{:S(2)}, u32[]{:S(2)}) collective-permute-start(bf16[2048,1536]{1,0:T(8,128)(2,1)} %constant_dynamic-slice_fusion.3), channel_id=1, source_target_pairs={{0,1},{1,0},{2,3},{3,2},{4,5},{5,4},{6,7},{7,6},{8,9},{9,8},{10,11... | collective-permute-start | bytes 18874376 | tf_op jit(solution)/shard_map/ppermute | solution.py:111
  117.4 30.4 %collective-permute-start.5 = (bf16[384,1536]{0,1:T(8,128)(2,1)}, bf16[384,1536]{0,1:T(8,128)(2,1)S(1)}, u32[]{:S(2)}, u32[]{:S(2)}) collective-permute-start(bf16[384,1536]{0,1:T(8,128)(2,1)} %collective-permute-done.3), channel_id=1, source_target_pairs={{0,8},{8,0},{1,9},{9,1},{2,10},{10,2},{3,11},{11,3},{4,12},{12,4},... | collective-permute-start | bytes 3538952 | tf_op jit(solution)/shard_map/ppermute | solution.py:111
  122.6 61.1 %collective-permute-start.10 = (bf16[384,1536]{1,0:T(8,128)(2,1)}, bf16[384,1536]{1,0:T(8,128)(2,1)S(1)}, u32[]{:S(2)}, u32[]{:S(2)}) collective-permute-start(bf16[384,1536]{1,0:T(8,128)(2,1)} %collective-permute-done.6), channel_id=1, source_target_pairs={{0,4},{4,0},{1,5},{5,1},{2,6},{6,2},{3,7},{7,3},{8,12},{12,8},{9,1... | collective-permute-start | bytes 3538952 | tf_op jit(solution)/shard_map/ppermute | solution.py:111
  124.1 60.6 %collective-permute-start.11 = (bf16[384,1536]{1,0:T(8,128)(2,1)S(1)}, bf16[384,1536]{1,0:T(8,128)(2,1)S(1)}, u32[]{:S(2)}, u32[]{:S(2)}) collective-permute-start(bf16[384,1536]{1,0:T(8,128)(2,1)S(1)} %collective-permute-done.9), channel_id=1, source_target_pairs={{0,8},{8,0},{1,9},{9,1},{2,10},{10,2},{3,11},{11,3},{4,12},{12,4},... | collective-permute-start | bytes 3538952 | tf_op jit(solution)/shard_map/ppermute | solution.py:111
  183.4 165.1 %all-gather.5.cloned.1.call-start = ((), (), s32[]{:S(2)}) async-start(), calls=%async_computation.6 | async-start | bytes 10616832 | tf_op jit(solution)/shard_map/all_gather | solution.py:180
  243.2 540.6 %reduce-scatter.7.cloned.1.call-start = ((), (), s32[]{:S(2)}) async-start(), calls=%async_computation.7 | async-start | bytes 21233664 | tf_op jit(solution)/shard_map/reduce_scatter | solution.py:191
  283.5 51.8 %collective-permute-start.15 = (bf16[2048,1536]{1,0:T(8,128)(2,1)}, bf16[2048,1536]{1,0:T(8,128)(2,1)}, u32[]{:S(2)}, u32[]{:S(2)}) collective-permute-start(bf16[2048,1536]{1,0:T(8,128)(2,1)} %constant_dynamic-slice_fusion.2), channel_id=1, source_target_pairs={{0,1},{1,0},{2,3},{3,2},{4,5},{5,4},{6,7},{7,6},{8,9},{9,8},{10,11... | collective-permute-start | bytes 18874376 | tf_op jit(solution)/shard_map/ppermute | solution.py:111
  476.8 313.3 %reduce-scatter.5.cloned.1.call-start = ((), (), s32[]{:S(2)}) async-start(), calls=%async_computation.5 | async-start | bytes 21233664 | tf_op jit(solution)/shard_map/reduce_scatter | solution.py:191
  533.4 375.3 %reduce-scatter.9.cloned.1.call-start = ((), (), s32[]{:S(2)}) async-start(), calls=%async_computation.8 | async-start | bytes 21233664 | tf_op jit(solution)/shard_map/reduce_scatter | solution.py:191
  561.1 27.3 %collective-permute-start.16 = (f32[2048,1536]{1,0:T(8,128)}, f32[2048,1536]{1,0:T(8,128)S(1)}, u32[]{:S(2)}, u32[]{:S(2)}) collective-permute-start(f32[2048,1536]{1,0:T(8,128)} %fusion.44), channel_id=1, source_target_pairs={{0,1},{1,0},{2,3},{3,2},{4,5},{5,4},{6,7},{7,6},{8,9},{9,8},{10,11... | collective-permute-start | bytes 37748744 | tf_op jit(solution)/shard_map/ppermute | solution.py:111
  658.2 395.7 %reduce-scatter.11.cloned.1.call-start = ((), (), s32[]{:S(2)}) async-start(), calls=%async_computation.9 | async-start | bytes 21233664 | tf_op jit(solution)/shard_map/reduce_scatter | solution.py:191
  1075.5 27.7 %collective-permute-start.19 = (bf16[384,1536]{1,0:T(8,128)(2,1)}, bf16[384,1536]{1,0:T(8,128)(2,1)}, u32[]{:S(2)}, u32[]{:S(2)}) collective-permute-start(bf16[384,1536]{1,0:T(8,128)(2,1)} %get-tuple-element.51), channel_id=1, source_target_pairs={{0,1},{1,0},{2,3},{3,2},{4,5},{5,4},{6,7},{7,6},{8,9},{9,8},{10,11... | collective-permute-start | bytes 3538952 | tf_op jit(solution)/shard_map/ppermute | solution.py:111
  1075.5 31.8 %collective-permute-start.20 = (bf16[384,1536]{1,0:T(8,128)(2,1)}, bf16[384,1536]{1,0:T(8,128)(2,1)}, u32[]{:S(2)}, u32[]{:S(2)}) collective-permute-start(bf16[384,1536]{1,0:T(8,128)(2,1)} %get-tuple-element.51), channel_id=1, source_target_pairs={{0,2},{2,0},{1,3},{3,1},{4,6},{6,4},{5,7},{7,5},{8,10},{10,8},{9,1... | collective-permute-start | bytes 3538952 | tf_op jit(solution)/shard_map/ppermute | solution.py:111
  1085.1 36.3 %collective-permute-start.26 = (bf16[384,1536]{1,0:T(8,128)(2,1)}, bf16[384,1536]{1,0:T(8,128)(2,1)}, u32[]{:S(2)}, u32[]{:S(2)}) collective-permute-start(bf16[384,1536]{1,0:T(8,128)(2,1)} %get-tuple-element.58), channel_id=1, source_target_pairs={{0,1},{1,0},{2,3},{3,2},{4,5},{5,4},{6,7},{7,6},{8,9},{9,8},{10,11... | collective-permute-start | bytes 3538952 | tf_op jit(solution)/shard_map/ppermute | solution.py:111
  1085.2 44.8 %collective-permute-start.27 = (bf16[384,1536]{1,0:T(8,128)(2,1)}, bf16[384,1536]{1,0:T(8,128)(2,1)}, u32[]{:S(2)}, u32[]{:S(2)}) collective-permute-start(bf16[384,1536]{1,0:T(8,128)(2,1)} %get-tuple-element.58), channel_id=1, source_target_pairs={{0,2},{2,0},{1,3},{3,1},{4,6},{6,4},{5,7},{7,5},{8,10},{10,8},{9,1... | collective-permute-start | bytes 3538952 | tf_op jit(solution)/shard_map/ppermute | solution.py:111
  1103.2 81.4 %collective-permute-start.29 = (bf16[384,1536]{1,0:T(8,128)(2,1)}, bf16[384,1536]{1,0:T(8,128)(2,1)}, u32[]{:S(2)}, u32[]{:S(2)}) collective-permute-start(bf16[384,1536]{1,0:T(8,128)(2,1)} %get-tuple-element.62), channel_id=1, source_target_pairs={{0,1},{1,0},{2,3},{3,2},{4,5},{5,4},{6,7},{7,6},{8,9},{9,8},{10,11... | collective-permute-start | bytes 3538952 | tf_op jit(solution)/shard_map/ppermute | solution.py:111
  1107.3 47.4 %collective-permute-start.30 = (bf16[384,1536]{1,0:T(8,128)(2,1)}, bf16[384,1536]{1,0:T(8,128)(2,1)}, u32[]{:S(2)}, u32[]{:S(2)}) collective-permute-start(bf16[384,1536]{1,0:T(8,128)(2,1)} %get-tuple-element.62), channel_id=1, source_target_pairs={{0,2},{2,0},{1,3},{3,1},{4,6},{6,4},{5,7},{7,5},{8,10},{10,8},{9,1... | collective-permute-start | bytes 3538952 | tf_op jit(solution)/shard_map/ppermute | solution.py:111
  1108.8 47.4 %collective-permute-start.21 = (bf16[384,1536]{1,0:T(8,128)(2,1)}, bf16[384,1536]{1,0:T(8,128)(2,1)}, u32[]{:S(2)}, u32[]{:S(2)}) collective-permute-start(bf16[384,1536]{1,0:T(8,128)(2,1)} %collective-permute-done.20), channel_id=1, source_target_pairs={{0,1},{1,0},{2,3},{3,2},{4,5},{5,4},{6,7},{7,6},{8,9},{9,8},{10,11... | collective-permute-start | bytes 3538952 | tf_op jit(solution)/shard_map/ppermute | solution.py:111
  1121.4 61.0 %collective-permute-start.23 = (bf16[384,1536]{1,0:T(8,128)(2,1)}, bf16[384,1536]{1,0:T(8,128)(2,1)S(1)}, u32[]{:S(2)}, u32[]{:S(2)}) collective-permute-start(bf16[384,1536]{1,0:T(8,128)(2,1)} %get-tuple-element.57), channel_id=1, source_target_pairs={{0,1},{1,0},{2,3},{3,2},{4,5},{5,4},{6,7},{7,6},{8,9},{9,8},{10,11... | collective-permute-start | bytes 3538952 | tf_op jit(solution)/shard_map/ppermute | solution.py:111
  1130.0 30.9 %collective-permute-start.28 = (bf16[384,1536]{1,0:T(8,128)(2,1)}, bf16[384,1536]{1,0:T(8,128)(2,1)S(1)}, u32[]{:S(2)}, u32[]{:S(2)}) collective-permute-start(bf16[384,1536]{1,0:T(8,128)(2,1)} %collective-permute-done.27), channel_id=1, source_target_pairs={{0,1},{1,0},{2,3},{3,2},{4,5},{5,4},{6,7},{7,6},{8,9},{9,8},{10,11... | collective-permute-start | bytes 3538952 | tf_op jit(solution)/shard_map/ppermute | solution.py:111
  1154.8 27.7 %collective-permute-start.24 = (bf16[384,1536]{1,0:T(8,128)(2,1)}, bf16[384,1536]{1,0:T(8,128)(2,1)S(1)}, u32[]{:S(2)}, u32[]{:S(2)}) collective-permute-start(bf16[384,1536]{1,0:T(8,128)(2,1)} %get-tuple-element.57), channel_id=1, source_target_pairs={{0,2},{2,0},{1,3},{3,1},{4,6},{6,4},{5,7},{7,5},{8,10},{10,8},{9,1... | collective-permute-start | bytes 3538952 | tf_op jit(solution)/shard_map/ppermute | solution.py:111
  1156.2 33.2 %collective-permute-start.31 = (bf16[384,1536]{1,0:T(8,128)(2,1)}, bf16[384,1536]{1,0:T(8,128)(2,1)S(1)}, u32[]{:S(2)}, u32[]{:S(2)}) collective-permute-start(bf16[384,1536]{1,0:T(8,128)(2,1)} %collective-permute-done.30), channel_id=1, source_target_pairs={{0,1},{1,0},{2,3},{3,2},{4,5},{5,4},{6,7},{7,6},{8,9},{9,8},{10,11... | collective-permute-start | bytes 3538952 | tf_op jit(solution)/shard_map/ppermute | solution.py:111
  (16 other events, 273.9 us)
Sparse Core Ops, SparseCore 0:
  183.5 81.9 all-gather.2
  267.7 80.7 all-gather.4
  476.9 141.0 reduce-scatter.6
  622.2 141.0 reduce-scatter.4
  767.5 141.0 reduce-scatter.8
  912.8 141.0 reduce-scatter.10
